TPU v7x, 8 devices: a whole 2x2x1 slice. The times are simulated.
8 devices in a mesh: dp: 1 (over z), tp: 8 (over y, x, core).
Axes of the slice: x: 2, y: 2, z: 1, core: 2. Of those that a mesh axis runs over, the one named last changes fastest.
Arguments:
- hidden: bfloat16 [16, 64, 2048], P('dp')
- tree_mask: int32 [16, 64, 64], P('dp')
- depth: int32 [16, 64], P('dp')
- ctx_len: int32 [16], P('dp')
- block_table: int32 [16, 12], P('dp')
- score_id: int32 [16, 64], P('dp')
- k_cache: bfloat16 [192, 16, 8, 64], P('dp', None, 'tp')
- v_cache: bfloat16 [192, 16, 8, 64], P('dp', None, 'tp')
- attn_norm: bfloat16 [2048], replicated
- w_q: bfloat16 [2048, 2048], P(None, 'tp')
- w_k: bfloat16 [2048, 512], P(None, 'tp')
- w_v: bfloat16 [2048, 512], P(None, 'tp')
- w_o: bfloat16 [2048, 2048], P('tp')
- mlp_norm: bfloat16 [2048], replicated
- w_gate: bfloat16 [2048, 8192], P(None, 'tp')
- w_up: bfloat16 [2048, 8192], P(None, 'tp')
- w_down: bfloat16 [8192, 2048], P('tp')
- final_norm: bfloat16 [2048], replicated
- w_lm: bfloat16 [2048, 128256], P(None, 'tp')
Outputs:
- output 1: float32 [16, 64], P('dp')
- output 2: float32 [16, 64], P('dp')
- output 3: bfloat16 [192, 16, 8, 64], P('dp', None, 'tp')
- output 4: bfloat16 [192, 16, 8, 64], P('dp', None, 'tp')
All inputs are finite; a program needn't handle non-finite values.
Results may differ from a plain program's by a relative error of at most 0.00334518.
Values are sent between devices in bfloat16 or wider.
A program may use at most 1 GiB of HBM per device.

v0:
```python
import jax
import jax.numpy as jnp
from jax import lax
from jax.sharding import PartitionSpec as P

RMS_EPS = 1e-5
ROPE_THETA = 500000


def rms_norm(values, gain):
    widened = values.astype(jnp.float32)
    scale = lax.rsqrt(jnp.mean(widened * widened, axis=-1, keepdims=True) + RMS_EPS)
    return (widened * scale * gain.astype(jnp.float32)).astype(jnp.bfloat16)


def rotate(values, positions):
    head_dim = values.shape[-1]
    half = head_dim // 2
    inv_freq = 1.0 / (ROPE_THETA ** (jnp.arange(half, dtype=jnp.float32) * (2.0 / head_dim)))
    angles = positions.astype(jnp.float32)[..., None] * inv_freq
    cosine = jnp.cos(angles)[..., None, :]
    sine = jnp.sin(angles)[..., None, :]
    first = values[..., :half]
    second = values[..., half:]
    return jnp.concatenate([first * cosine - second * sine, second * cosine + first * sine], axis=-1)


def tree_attention(query, key_new, val_new, key_old, val_old, tree_mask, ctx_len):
    scale = query.shape[-1] ** -0.5
    span = key_old.shape[1]
    score_old = jnp.einsum("btkgh,bskh->btkgs", query, key_old, preferred_element_type=jnp.float32) * scale
    seen_old = jnp.arange(span)[None, :] < ctx_len[:, None]
    score_old = jnp.where(seen_old[:, None, None, None, :], score_old, -jnp.inf)
    score_new = jnp.einsum("btkgh,bjkh->btkgj", query, key_new, preferred_element_type=jnp.float32) * scale
    score_new = jnp.where((tree_mask > 0)[:, :, None, None, :], score_new, -jnp.inf)
    top = jnp.maximum(jnp.max(score_old, axis=-1), jnp.max(score_new, axis=-1))[..., None]
    prob_old = jnp.exp(score_old - top)
    prob_new = jnp.exp(score_new - top)
    total = jnp.sum(prob_old, axis=-1) + jnp.sum(prob_new, axis=-1)
    mixed = jnp.einsum("btkgs,bskh->btkgh", prob_old.astype(jnp.bfloat16), val_old, preferred_element_type=jnp.float32)
    mixed = mixed + jnp.einsum("btkgj,bjkh->btkgh", prob_new.astype(jnp.bfloat16), val_new, preferred_element_type=jnp.float32)
    return (mixed / total[..., None]).astype(jnp.bfloat16)


def write_cache(cache, table, ctx_len, new_rows):
    page_size = cache.shape[1]
    slots = ctx_len[:, None] + jnp.arange(new_rows.shape[1])[None, :]
    slot_blocks = jnp.take_along_axis(table, slots // page_size, axis=1)
    return cache.at[slot_blocks, slots % page_size].set(new_rows)


def layer_and_logits(hidden, tree_mask, depth, ctx_len, block_table, k_cache, v_cache, attn_norm, w_q, w_k, w_v, w_o, mlp_norm, w_gate, w_up, w_down, final_norm, w_lm):
    requests = hidden.shape[0]
    nodes = hidden.shape[1]
    page_size = k_cache.shape[1]
    kv_local = k_cache.shape[2]
    head_dim = k_cache.shape[3]
    span = block_table.shape[1] * page_size
    heads_local = w_q.shape[1] // head_dim
    normed = rms_norm(hidden, attn_norm)
    positions = ctx_len[:, None] + depth
    query = jnp.dot(normed, w_q, preferred_element_type=jnp.float32).reshape(requests, nodes, heads_local, head_dim)
    query = rotate(query, positions).astype(jnp.bfloat16).reshape(requests, nodes, kv_local, heads_local // kv_local, head_dim)
    key_new = jnp.dot(normed, w_k, preferred_element_type=jnp.float32).reshape(requests, nodes, kv_local, head_dim)
    key_new = rotate(key_new, positions).astype(jnp.bfloat16)
    val_new = jnp.dot(normed, w_v, preferred_element_type=jnp.float32).astype(jnp.bfloat16).reshape(requests, nodes, kv_local, head_dim)
    key_old = k_cache[block_table].reshape(requests, span, kv_local, head_dim)
    val_old = v_cache[block_table].reshape(requests, span, kv_local, head_dim)
    attended = tree_attention(query, key_new, val_new, key_old, val_old, tree_mask, ctx_len).reshape(requests, nodes, heads_local * head_dim)
    attn_sum = lax.psum(jnp.dot(attended, w_o, preferred_element_type=jnp.float32).astype(jnp.bfloat16), "tp")
    residual = (hidden.astype(jnp.float32) + attn_sum.astype(jnp.float32)).astype(jnp.bfloat16)
    normed_mlp = rms_norm(residual, mlp_norm)
    gate = jnp.dot(normed_mlp, w_gate, preferred_element_type=jnp.float32)
    upper = jnp.dot(normed_mlp, w_up, preferred_element_type=jnp.float32)
    product = (jax.nn.silu(gate) * upper).astype(jnp.bfloat16)
    mlp_sum = lax.psum(jnp.dot(product, w_down, preferred_element_type=jnp.float32).astype(jnp.bfloat16), "tp")
    layer_out = (residual.astype(jnp.float32) + mlp_sum.astype(jnp.float32)).astype(jnp.bfloat16)
    logits = jnp.dot(rms_norm(layer_out, final_norm), w_lm, preferred_element_type=jnp.float32)
    return logits, key_new, val_new


def solution(mesh):
    def group_step(hidden, tree_mask, depth, ctx_len, block_table, score_id, k_cache, v_cache, attn_norm, w_q, w_k, w_v, w_o, mlp_norm, w_gate, w_up, w_down, final_norm, w_lm):
        logits, key_new, val_new = layer_and_logits(hidden, tree_mask, depth, ctx_len, block_table, k_cache, v_cache, attn_norm, w_q, w_k, w_v, w_o, mlp_norm, w_gate, w_up, w_down, final_norm, w_lm)
        vocab_local = logits.shape[-1]
        global_top = lax.pmax(jnp.max(logits, axis=-1), "tp")
        part_sum = jnp.sum(jnp.exp(logits - global_top[..., None]), axis=-1)
        local_id = score_id - lax.axis_index("tp") * vocab_local
        inside = (local_id >= 0) & (local_id < vocab_local)
        picked = jnp.take_along_axis(logits, jnp.clip(local_id, 0, vocab_local - 1)[..., None], axis=-1)[..., 0]
        summed = lax.psum(jnp.stack([part_sum, jnp.where(inside, picked, 0.0)]), "tp")
        log_norm = global_top + jnp.log(summed[0])
        log_prob = summed[1] - log_norm
        return log_norm, log_prob, write_cache(k_cache, block_table, ctx_len, key_new), write_cache(v_cache, block_table, ctx_len, val_new)

    request_spec = P("dp", None, None)
    node_spec = P("dp", None)
    cache_spec = P("dp", None, "tp", None)
    shared_spec = P(None)
    column_spec = P(None, "tp")
    row_spec = P("tp", None)
    in_specs = (request_spec, request_spec, node_spec, P("dp"), node_spec, node_spec, cache_spec, cache_spec, shared_spec, column_spec, column_spec, column_spec, row_spec, shared_spec, column_spec, column_spec, row_spec, shared_spec, column_spec)
    out_specs = (node_spec, node_spec, cache_spec, cache_spec)
    return jax.shard_map(group_step, mesh=mesh, in_specs=in_specs, out_specs=out_specs, check_vma=False)
```

profile of v0, /device:TPU:0, one launch (start us, length us, event | category | flops | bytes accessed | tf_op | source)
XLA Modules:
  0.0 413.1 jit_solution(1187809131715738789)
XLA Ops:
  7.2 0.0 copy-start
  7.2 0.0 all-reduce.3.cloned.1.call-start
  7.3 0.8 iota_compare_fusion
  8.1 0.8 bitcast_or_fusion
  8.9 0.7 convert_element_type.84
  9.6 0.7 compare_select_fusion.4
  10.3 0.1 reshape.320
  10.4 3.1 fusion.5
  13.5 0.1 reshape.387
  13.5 7.1 %gather_fusion.3 = s32[1024]{0:T(1024)S(1)} fusion(s32[16,12]{1,0:T(8,128)S(1)} %copy-done.2, s32[1024]{0:T(1024)S(1)} %reshape.387), kind=kCustom, calls=%fused_computation.clone | custom fusion | bytes 16384 | tf_op jit(solution)/shard_map/jit(take_along_axis)/gather | solution.py:48
  20.6 0.1 reshape.390
  20.7 0.1 broadcast_compare_fusion
  20.8 0.9 copy.35
  21.6 4.4 %fusion.59 = bf16[16,64,64]{2,1,0:T(8,128)(2,1)} fusion(bf16[16,64,2048]{2,1,0:T(8,128)(2,1)} %param.21, f32[2048]{0:T(1024)S(1)} %convert_element_type.84, f32[16,64]{1,0:T(8,128)S(1)} %add_rsqrt_fusion.2, bf16[2048,64]{0,1:T(8,128)(2,1)S(1)} %copy-done.27), kind=kOutput, calls=%fused_computation.64 | convolution fusion | flops 276889600 | bytes 4599808 | tf_op jit(solution)/shard_map/dot_general | solution.py:66
  26.0 2.2 fusion.56
  28.3 0.7 fusion.83
  28.9 3.0 multiply_cosine_fusion
  32.0 1.8 fusion.72
  33.8 0.6 copy.31
  34.4 0.6 copy.30
  35.1 0.8 gather_fusion
  35.8 1.6 gather_fusion.1
  37.5 4.8 %fusion.34 = f32[16,64,256]{2,1,0:T(8,128)} fusion(bf16[16,64,2048]{2,1,0:T(8,128)(2,1)} %param.21, f32[2048]{0:T(1024)} %copy-done.19, f32[16,64]{1,0:T(8,128)} %copy-done.20, bf16[2048,256]{1,0:T(8,128)(2,1)} %param.30), kind=kOutput, calls=%fused_computation.47 | convolution fusion | flops 1082130432 | bytes 6303744 | tf_op jit(solution)/shard_map/dot_general | solution.py:62
  42.3 3.2 reshape.295
  45.6 3.6 fusion.105
  49.2 0.8 subtract_convert_fusion
  50.1 0.2 copy-done.5
  50.3 1.4 bitcast_reduce_fusion
  51.7 1.2 fusion.106
  52.9 0.5 fusion.45
  53.5 1.4 fusion.26
  54.9 2.3 fusion.37
  57.3 0.6 fusion.39
  57.9 3.3 convolution_convert_fusion
  61.2 0.0 all-reduce.3.cloned.1.call-update
  61.2 0.0 all-reduce.5.cloned.1.call-start
  61.3 72.2 %all-reduce.3.cloned.1.call-done = bf16[16,64,2048]{2,1,0:T(8,128)(2,1)} async-done(((bf16[16,64,2048]{2,1,0:T(8,128)(2,1)}), bf16[16,64,2048]{2,1,0:T(8,128)(2,1)}) %all-reduce.3.cloned.1.call-update) | async-done | bytes 4194320 | tf_op jit(solution)/shard_map/psum | solution.py:70
  133.5 5.6 %fusion.9 = (f32[16,64]{1,0:T(8,128)S(1)}, bf16[16,64,2048]{2,1,0:T(8,128)(2,1)S(1)}) fusion(bf16[16,64,2048]{2,1,0:T(8,128)(2,1)} %all-reduce.3.cloned.1.call-done, bf16[16,64,2048]{2,1,0:T(8,128)(2,1)} %param.21), kind=kLoop, calls=%fused_computation.24 | loop fusion | flops 14679040 | bytes 12587008 | tf_op jit(solution)/shard_map/reduce_sum | solution.py:12
  139.1 2.0 copy-done.3
  141.1 6.4 %fusion.16 = f32[16,64,1024]{2,1,0:T(8,128)} fusion(bf16[2048,1024]{1,0:T(8,128)(2,1)S(1)} %copy-done.26, bf16[16,64,2048]{2,1,0:T(8,128)(2,1)S(1)} %get-tuple-element.12, f32[2048]{0:T(1024)S(1)} %convert_element_type.96, f32[16,64]{1,0:T(8,128)S(1)} %add_rsqrt_fusion.1), kind=kOutput, calls=%fused_computation.30 | convolution fusion | flops 4303355904 | bytes 12595200 | tf_op jit(solution)/shard_map/dot_general | solution.py:74
  147.4 15.6 %fusion.23 = bf16[16,64,2048]{2,1,0:T(8,128)(2,1)} fusion(bf16[1024,2048]{1,0:T(8,128)(2,1)} %param.37, f32[16,64,1024]{2,1,0:T(8,128)} %fusion.16, bf16[2048,1024]{1,0:T(8,128)(2,1)} %param.35, bf16[16,64,2048]{2,1,0:T(8,128)(2,1)} %copy-done.3, f32[2048]{0:T(1024)S(1)} %convert_element_type.96, f32[16,64]{1,0:T(8,128)S(1)} %add_rsqrt_fusion.1), kind=kOutput, calls=%fused_computation.42 | convolution fusion | flops 8606711808 | bytes 20983808 | tf_op jit(solution)/shard_map/dot_general | solution.py:76
  163.0 0.0 copy-start.25
  163.1 0.0 all-reduce.5.cloned.1.call-update
  163.1 0.6 copy-done.23
  163.7 0.0 copy-done.17
  163.8 0.1 reshape.338
  163.9 0.1 multiply_reduce_fusion
  163.9 0.1 and_reduce_fusion
  164.0 0.1 reshape.348
  164.1 0.1 pad_maximum_fusion.1
  164.2 0.2 copy.61
  164.4 3.6 scatter_fusion.1
  168.0 1.5 copy.46
  169.5 3.6 scatter_fusion
  173.1 1.5 copy.45
  174.5 58.1 %all-reduce.5.cloned.1.call-done = bf16[16,64,2048]{2,1,0:T(8,128)(2,1)} async-done(((bf16[16,64,2048]{2,1,0:T(8,128)(2,1)}), bf16[16,64,2048]{2,1,0:T(8,128)(2,1)}) %all-reduce.5.cloned.1.call-update) | async-done | bytes 4194320 | tf_op jit(solution)/shard_map/psum | solution.py:76
  232.6 4.9 %fusion.2 = f32[16,64]{1,0:T(8,128)S(1)} fusion(bf16[16,64,2048]{2,1,0:T(8,128)(2,1)} %all-reduce.5.cloned.1.call-done, bf16[16,64,2048]{2,1,0:T(8,128)(2,1)} %copy-done.3), kind=kLoop, calls=%fused_computation.17 | loop fusion | flops 14679040 | bytes 8392704 | tf_op jit(solution)/shard_map/reduce_sum | solution.py:12
  237.5 83.6 %fusion.107 = (f32[16,64]{1,0:T(8,128)S(1)}, f32[16,64,16032]{2,1,0:T(8,128)}) fusion(bf16[2048,16032]{0,1:T(8,128)(2,1)} %param.39, f32[2048]{0:T(1024)S(1)} %convert_element_type.103, f32[16,64]{1,0:T(8,128)S(1)} %add_rsqrt_fusion, bf16[16,64,2048]{2,1,0:T(8,128)(2,1)} %all-reduce.5.cloned.1.call-done, bf16[16,64,2048]{2,1,0:T(8,128)(2,1)} %copy-done.3), kind=kOutput, calls=%fused_computation.149 | convolution fusion | flops 67276275712 | bytes 139739136 | tf_op jit(solution)/shard_map/dot_general | solution.py:78
  321.1 22.3 %pmax.7 = f32[16,64]{1,0:T(8,128)S(1)} all-reduce(f32[16,64]{1,0:T(8,128)S(1)} %get-tuple-element.29), channel_id=1, replica_groups=mesh['dp'=1,'tp'=8] {'tp'}, use_global_device_ids=true, to_apply=%region_10.11 | all-reduce | flops 1024 | bytes 8192 | tf_op jit(solution)/shard_map/pmax | solution.py:86
  343.4 16.5 %gather_fusion.2 = f32[1024]{0:T(1024)S(1)} fusion(f32[16,64,16032]{2,1,0:T(8,128)} %get-tuple-element.30, s32[1024]{0:T(1024)S(1)} %reshape.338), kind=kCustom, calls=%fused_computation.3 | custom fusion | bytes 20480 | tf_op jit(solution)/shard_map/jit(take_along_axis)/gather | solution.py:90
  360.0 20.9 %exponential_reduce_fusion = f32[16,64]{1,0:T(8,128)S(1)} fusion(f32[16,64,16032]{2,1,0:T(8,128)} %get-tuple-element.30, f32[16,64]{1,0:T(8,128)S(1)} %pmax.7), kind=kLoop, calls=%fused_computation.6 | loop fusion | flops 32832512 | bytes 65675264 | tf_op jit(solution)/shard_map/reduce_sum | solution.py:87
  380.9 0.1 gather.18
  381.0 24.2 %psum.23 = f32[2,16,64]{2,1,0:T(8,128)S(1)} all-reduce(f32[2,16,64]{2,1,0:T(8,128)S(1)} %pad_maximum_fusion.4), channel_id=1, replica_groups=mesh['dp'=1,'tp'=8] {'tp'}, use_global_device_ids=true, to_apply=%region_12.13 | all-reduce | flops 2048 | bytes 16384 | tf_op jit(solution)/shard_map/psum | solution.py:91
  405.2 0.6 fusion.84
  (69 shorter events, 0.3 us)
Async XLA Ops:
  7.2 50.7 %copy-start = (bf16[256,2048]{1,0:T(8,128)(2,1)S(1)}, bf16[256,2048]{1,0:T(8,128)(2,1)}, u32[]{:S(2)}) copy-start(bf16[256,2048]{1,0:T(8,128)(2,1)} %param.33) | copy-start | bytes 3145732
  7.2 6.4 %copy-start.2 = (s32[16,12]{1,0:T(8,128)S(1)}, s32[16,12]{1,0:T(8,128)}, u32[]{:S(2)}) copy-start(s32[16,12]{1,0:T(8,128)} %param.25) | copy-start | bytes 2308
  7.2 126.3 %all-reduce.3.cloned.1.call-start = ((), (), s32[]{:S(2)}) async-start(), calls=%async_computation | async-start | bytes 8388608 | tf_op jit(solution)/shard_map/psum | solution.py:70
  9.6 16.4 %copy-start.19 = (f32[2048]{0:T(1024)}, f32[2048]{0:T(1024)S(1)}, u32[]{:S(2)}) copy-start(f32[2048]{0:T(1024)S(1)} %convert_element_type.84) | copy-start | bytes 24580
  13.5 12.5 %copy-start.20 = (f32[16,64]{1,0:T(8,128)}, f32[16,64]{1,0:T(8,128)S(1)}, u32[]{:S(2)}) copy-start(f32[16,64]{1,0:T(8,128)S(1)} %add_rsqrt_fusion.2) | copy-start | bytes 12292
  13.5 7.1 %copy-start.10 = (s32[16,64,64]{2,1,0:T(8,128)S(1)}, s32[16,64,64]{2,1,0:T(8,128)}, u32[]{:S(2)}) copy-start(s32[16,64,64]{2,1,0:T(8,128)} %param.22) | copy-start | bytes 786436
  13.5 8.1 %copy-start.27 = (bf16[2048,64]{0,1:T(8,128)(2,1)S(1)}, bf16[2048,64]{0,1:T(8,128)(2,1)}, u32[]{:S(2)}) copy-start(bf16[2048,64]{0,1:T(8,128)(2,1)} %param.32) | copy-start | bytes 786436
  21.6 4.4 %copy-start.4 = (bf16[16,64,2048]{2,1,0:T(8,128)(2,1)S(1)}, bf16[16,64,2048]{2,1,0:T(8,128)(2,1)}, u32[]{:S(2)}) copy-start(bf16[16,64,2048]{2,1,0:T(8,128)(2,1)} %param.21) | copy-start | bytes 12582916
  21.6 4.4 %copy-start.28 = (bf16[2048,64]{0,1:T(8,128)(2,1)S(1)}, bf16[2048,64]{0,1:T(8,128)(2,1)}, u32[]{:S(2)}) copy-start(bf16[2048,64]{0,1:T(8,128)(2,1)} %param.31) | copy-start | bytes 786436
  26.0 2.2 copy-start.18
  26.0 2.2 copy-start.21
  26.0 7.7 %copy-start.12 = (bf16[192,16,1,64]{0,3,2,1:T(8,128)(2,1)S(1)}, bf16[192,16,1,64]{0,3,2,1:T(8,128)(2,1)}, u32[]{:S(2)}) copy-start(bf16[192,16,1,64]{0,3,2,1:T(8,128)(2,1)} %param.27) | copy-start | bytes 1179652
  26.0 8.4 %copy-start.13 = (bf16[192,16,1,64]{0,3,2,1:T(8,128)(2,1)S(1)}, bf16[192,16,1,64]{0,3,2,1:T(8,128)(2,1)}, u32[]{:S(2)}) copy-start(bf16[192,16,1,64]{0,3,2,1:T(8,128)(2,1)} %param.28) | copy-start | bytes 1179652
  45.5 3.7 copy-start.6
  45.5 3.7 copy-start.7
  49.2 1.1 copy-start.5
  50.1 1.6 copy-start.8
  50.1 1.6 copy-start.11
  54.9 2.3 copy-start.14
  57.9 3.4 copy-start.22
  61.2 171.4 %all-reduce.5.cloned.1.call-start = ((), (), s32[]{:S(2)}) async-start(), calls=%async_computation.1 | async-start | bytes 8388608 | tf_op jit(solution)/shard_map/psum | solution.py:76
  133.5 7.6 %copy-start.26 = (bf16[2048,1024]{1,0:T(8,128)(2,1)S(1)}, bf16[2048,1024]{1,0:T(8,128)(2,1)}, u32[]{:S(2)}) copy-start(bf16[2048,1024]{1,0:T(8,128)(2,1)} %param.36) | copy-start | bytes 12582916
  139.1 2.0 copy-start.3
  163.0 0.7 copy-start.23
  163.0 0.7 copy-start.17
  163.0 0.8 copy-start.16
  163.0 0.8 copy-start.25
  163.0 0.9 copy-start.24
  163.1 1.0 copy-start.9
  163.1 1.3 copy-start.15
  359.9 45.8 %copy-start.1 = (bf16[256,2048]{1,0:T(8,128)(2,1)S(1)}, bf16[256,2048]{1,0:T(8,128)(2,1)}, u32[]{:S(2)}) copy-start(bf16[256,2048]{1,0:T(8,128)(2,1)} %param.33) | copy-start | bytes 3145732
Sparse Core Ops, SparseCore 0:
  61.3 72.0 all-reduce.2
  163.2 69.3 all-reduce.4
where the time goes:
time: 421 us; the launch traced here: 413 us
  waiting for transfers between devices  130 us (31%)
  matrix products  126 us (30%)
  local copies, waits for them, and re-layouts  48.7 us (12%)
  other arithmetic  46.8 us (11%)
  blocking collectives  46.5 us (11%)
  between operations  15 us (4%)
    dot_general x1, matrix products, layer_and_logits(): jnp.dot(rms_norm(layer_out, final_norm), w_lm, preferred_element_type=jnp...  83.6 us
    psum x1, waiting for transfers between devices, layer_and_logits(): lax.psum(jnp.dot(attended, w_o, preferred_element_type=jnp.float32).astyp...  72.2 us
    psum x1, waiting for transfers between devices, layer_and_logits(): lax.psum(jnp.dot(product, w_down, preferred_element_type=jnp.float32).ast...  58.1 us
    psum x1, blocking collectives, group_step(): lax.psum(jnp.stack([part_sum, jnp.where(inside, picked, 0.0)]), 'tp')  24.2 us
    pmax x1, blocking collectives, group_step(): global_top = lax.pmax(jnp.max(logits, axis=-1), 'tp')  22.3 us
    reduce_sum x1, other arithmetic, group_step(): part_sum = jnp.sum(jnp.exp(logits - global_top[..., None]), axis=-1)  20.9 us
    gather x3, local copies, waits for them, and re-layouts, group_step(): jnp.take_along_axis(logits, jnp.clip(local_id, 0, vocab_local - 1)[..., N...  16.6 us
    dot_general x1, matrix products, layer_and_logits(): jnp.dot(product, w_down, preferred_element_type=jnp.float32)  15.6 us
  transfers between devices with their start and end apart: 2, of which 2 were waited for; matrix products, arithmetic and copies ran while one was open for 3% of the time, Pallas kernels for 0%

commit v1 on v0

v1 whole, which is shorter than its diff:
```python
import functools

import jax
import jax.numpy as jnp
import numpy as np
from jax import lax
from jax.experimental import pallas as pl
from jax.experimental.pallas import tpu as pltpu
from jax.sharding import PartitionSpec as P

RMS_EPS = 1e-5
ROPE_THETA = 500000
DIM = 2048
ROWS = 1024
NODES = 64
PAGES = 12
PAGE = 16
SPAN = PAGES * PAGE
HD = 64
FFN = 1024
VOCAB = 16032
TILE = 1024
FULL_TILES = 15
LAST = 640
TAIL_AT = 16000
CHUNKS = 2
CR = ROWS // CHUNKS
HALF = CR // 2
BR = CR // 8
MESH = pl.DeviceIdType.MESH
F32 = jnp.float32
BF16 = jnp.bfloat16


def rope_table():
    half = HD // 2
    freq = (np.float32(1.0) / np.power(np.float32(ROPE_THETA), np.arange(half, dtype=np.float32) * np.float32(2.0 / HD))).astype(np.float32)
    angle = (np.arange(SPAN, dtype=np.float32)[:, None] * freq[None, :]).astype(np.float32).astype(np.float64)
    cos = np.tile(np.cos(angle), (1, 4)).astype(np.float32)
    sin = np.sin(angle)
    sin = np.concatenate([-sin, sin, -sin, sin], axis=1).astype(np.float32)
    table = np.concatenate([cos, sin], axis=1)
    high = table.astype(jnp.bfloat16)
    rest = table - high.astype(np.float32)
    mid = rest.astype(jnp.bfloat16)
    low = (rest - mid.astype(np.float32)).astype(jnp.bfloat16)
    return np.concatenate([high, mid, low], axis=1)


def normalize(values, gain):
    scale = lax.rsqrt(jnp.mean(values * values, axis=-1, keepdims=True) + RMS_EPS)
    return (values * scale * gain).astype(BF16)


def dot(a, b):
    return jnp.dot(a, b, preferred_element_type=F32)


def dot_nt(a, b):
    return lax.dot_general(a, b, (((1,), (1,)), ((), ())), preferred_element_type=F32)


def dot_tn(a, b):
    return lax.dot_general(a, b, (((0,), (0,)), ((), ())), preferred_element_type=F32)


def attention_kernel(group, ctx_ref, bt_ref, hid_ref, depth_ref, mask_ref, gain_ref, wq_ref, wkv_ref, table_ref, kv_ref, att_ref, kvout_ref, old_ref):
    step = pl.program_id(0)
    normed = normalize(hid_ref[...].astype(F32), gain_ref[...].astype(F32))
    q_all = dot(normed, wq_ref[...])
    kv_all = dot(normed, wkv_ref[...])
    lane = lax.broadcasted_iota(jnp.int32, (1, 128), 1)
    low = lane < 64
    first = (lane % 64) < 32

    def rope(values, cosine, sine):
        swapped = jnp.where(first, pltpu.roll(values, 96, 1), pltpu.roll(values, 32, 1))
        return values * cosine + swapped * sine

    for i in range(group):
        b = step * group + i
        ctx = ctx_ref[b]
        rows = slice(i * NODES, (i + 1) * NODES)
        position = depth_ref[i] + ctx
        hot = (lax.broadcasted_iota(jnp.int32, (SPAN, NODES), 0) == position).astype(F32).astype(BF16)
        looked = dot_tn(hot, table_ref[...])
        both = looked[:, :256] + looked[:, 256:512] + looked[:, 512:]
        cosine, sine = both[:, :128], both[:, 128:]
        q01 = (rope(q_all[rows, :128], cosine, sine) * 0.125).astype(BF16)
        q23 = (rope(q_all[rows, 128:], cosine, sine) * 0.125).astype(BF16)
        kv_new = rope(kv_all[rows], jnp.where(low, cosine, 1.0), jnp.where(low, sine, 0.0)).astype(BF16)
        for p in range(PAGES):
            old_ref[i, p * PAGE:(p + 1) * PAGE, :] = kv_ref[bt_ref[b, p]].astype(F32)
        slot = lax.broadcasted_iota(jnp.int32, (SPAN, NODES), 0)
        node = lax.broadcasted_iota(jnp.int32, (SPAN, NODES), 1)
        place = (slot - node == ctx).astype(F32).astype(BF16)
        shifted = dot(place, kv_new)
        slot_col = lax.broadcasted_iota(jnp.int32, (SPAN, 128), 0)
        fresh = (slot_col >= ctx) & (slot_col < ctx + NODES)
        merged = jnp.where(fresh, shifted, old_ref[i])
        merged16 = merged.astype(BF16)
        for p in range(PAGES):
            kvout_ref[bt_ref[b, p]] = merged16[p * PAGE:(p + 1) * PAGE]
        turned = pltpu.roll(merged, 64, 1)
        k_even = jnp.where(low, merged, 0.0).astype(BF16)
        v_odd = jnp.where(low, 0.0, merged).astype(BF16)
        v_even = jnp.where(low, turned, 0.0).astype(BF16)
        k_odd = jnp.where(low, 0.0, turned).astype(BF16)
        tree = dot_nt(mask_ref[i].astype(F32).astype(BF16), place)
        slot_row = lax.broadcasted_iota(jnp.int32, (NODES, SPAN), 1)
        seen = (slot_row < ctx) | (tree > 0.5)

        def head(query, keys):
            score = jnp.where(seen, dot_nt(query, keys), -jnp.inf)
            weight = jnp.exp(score - jnp.max(score, axis=-1, keepdims=True))
            return weight.astype(BF16), jnp.sum(weight, axis=-1, keepdims=True)

        for pair, query in enumerate((q01, q23)):
            w_even, t_even = head(query, k_even)
            w_odd, t_odd = head(query, k_odd)
            mixed = dot(w_even, v_even) + dot(w_odd, v_odd)
            att_ref[rows, pair * 128:(pair + 1) * 128] = (mixed / jnp.where(low, t_even, t_odd)).astype(BF16)


def attention(hidden, tree_mask, depth, ctx_len, block_table, kv_cache, attn_norm, w_q, w_kv, table):
    group = 4
    grid = (hidden.shape[0] // (group * NODES),)
    spec = pltpu.PrefetchScalarGridSpec(
        num_scalar_prefetch=2,
        grid=grid,
        in_specs=[
            pl.BlockSpec((group * NODES, DIM), lambda i, *_: (i, 0)),
            pl.BlockSpec((group, 1, NODES), lambda i, *_: (i, 0, 0)),
            pl.BlockSpec((group, NODES, NODES), lambda i, *_: (i, 0, 0)),
            pl.BlockSpec((1, DIM), lambda i, *_: (0, 0)),
            pl.BlockSpec((DIM, 256), lambda i, *_: (0, 0)),
            pl.BlockSpec((DIM, 128), lambda i, *_: (0, 0)),
            pl.BlockSpec(table.shape, lambda i, *_: (0, 0)),
            pl.BlockSpec(kv_cache.shape, lambda i, *_: (0, 0, 0)),
        ],
        out_specs=[
            pl.BlockSpec((group * NODES, 256), lambda i, *_: (i, 0)),
            pl.BlockSpec(kv_cache.shape, lambda i, *_: (0, 0, 0)),
        ],
        scratch_shapes=[pltpu.VMEM((group, SPAN, 128), F32)],
    )
    return pl.pallas_call(
        functools.partial(attention_kernel, group),
        grid_spec=spec,
        out_shape=[jax.ShapeDtypeStruct((hidden.shape[0], 256), BF16), jax.ShapeDtypeStruct(kv_cache.shape, BF16)],
        compiler_params=pltpu.CompilerParams(vmem_limit_bytes=40 * 2**20),
        name="attention",
    )(ctx_len, block_table, hidden, depth, tree_mask, attn_norm, w_q, w_kv, table, kv_cache)


def layer_kernel(att, wo, hid, mgain, wg_hbm, wu_hbm, wd_hbm, fgain, wlm, wtail, sid, ln_ref, lp_ref,
                 wg, wu, wd, wbuf, psib, pown, s1buf, s2buf, mfull, hown, pact, mrun, srun, prun, stat,
                 load_sem, tile_sem, s1_send, s1_recv, s2_send, s2_recv, ag_send, ag_recv, fw_send, fw_recv, fin_send, fin_recv):
    me = lax.axis_index("tp")
    core = me % 2
    chip = me // 2
    cx = chip % 2
    cy = chip // 2
    sib = me + 1 - 2 * core
    far = (chip + 1 - 2 * cx, chip + 2 - 4 * cy, 3 - chip)

    def peer(rel):
        return 2 * far[rel] + core

    def remote(src, dst, ssem, rsem, target):
        return pltpu.make_async_remote_copy(src_ref=src, dst_ref=dst, send_sem=ssem, recv_sem=rsem, device_id={"tp": target}, device_id_type=MESH)

    barrier = pltpu.get_barrier_semaphore()
    for off in range(1, 8):
        pl.semaphore_signal(barrier, inc=1, device_id={"tp": (me + off) % 8}, device_id_type=MESH)

    loads = [
        pltpu.make_async_copy(wg_hbm, wg, load_sem.at[0]),
        pltpu.make_async_copy(wu_hbm, wu, load_sem.at[1]),
        pltpu.make_async_copy(wd_hbm, wd, load_sem.at[2]),
    ]

    def own_rows(c):
        return c * CR + (core * 4 + chip) * BR

    hid_loads = [
        pltpu.make_async_copy(hid.at[pl.ds(pl.multiple_of(own_rows(c), BR), BR)], hown.at[pl.ds(c * BR, BR)], load_sem.at[3 + c])
        for c in range(CHUNKS)
    ]
    for copy in hid_loads + loads:
        copy.start()

    def tile_copy(t, j):
        return pltpu.make_async_copy(wlm.at[:, pl.ds(pl.multiple_of(j * TILE, TILE), TILE)], wbuf.at[t % 3], tile_sem.at[t % 3])

    def last_copy(t):
        return pltpu.make_async_copy(wlm.at[:, pl.ds(FULL_TILES * TILE, LAST)], wbuf.at[t % 3, :, pl.ds(0, LAST)], tile_sem.at[t % 3])

    tile_copy(0, 0).start()
    tile_copy(1, 1).start()

    mrun[...] = jnp.full_like(mrun, -jnp.inf)
    srun[...] = jnp.zeros_like(srun)
    prun[...] = jnp.zeros_like(prun)

    def half_rows(c, which):
        return pl.ds(pl.multiple_of(c * CR + which * HALF, HALF), HALF)

    def slab(c):
        return pl.ds(c * HALF, HALF)

    def first_copy(s, c):
        return remote(psib.at[s, slab(c)], s1buf.at[s, slab(c)], s1_send.at[s, c], s1_recv.at[s, c], sib)

    def project(c):
        psib[0, slab(c)] = dot(att[half_rows(c, 1 - core)], wo[...]).astype(BF16)
        if c == 0:
            pl.semaphore_wait(barrier, 7)
        first_copy(0, c).start()
        pown[0, slab(c)] = dot(att[half_rows(c, core)], wo[...]).astype(BF16)

    def second_copy(s, c, rel):
        block = pl.ds(pl.multiple_of(c * HALF + far[rel] * BR, BR), BR)
        return remote(pown.at[s, block], s2buf.at[s, c, rel], s2_send.at[s, c, rel], s2_recv.at[s, c, rel], peer(rel))

    def pair_sum(s, c):
        first_copy(s, c).wait_recv()
        pown[s, slab(c)] = (pown[s, slab(c)].astype(F32) + s1buf[s, slab(c)].astype(F32)).astype(BF16)
        for rel in range(3):
            second_copy(s, c, rel).start()

    def block_rows(c, k, q):
        return pl.ds(pl.multiple_of(c * CR + (k * 4 + q) * BR, BR), BR)

    def gather_copy(s, c, rel, rows):
        target = sib if rel == 3 else peer(rel)
        return remote(mfull.at[s, rows], mfull.at[s, rows], ag_send.at[s, c, rel], ag_recv.at[s, c, rel], target)

    def forward_copy(s, c, rel, rows):
        return remote(mfull.at[s, rows], mfull.at[s, rows], fw_send.at[s, c, rel], fw_recv.at[s, c, rel], sib)

    def finish_sum(s, c):
        for rel in range(3):
            second_copy(s, c, rel).wait_recv()
        total = pown[s, pl.ds(pl.multiple_of(c * HALF + chip * BR, BR), BR)].astype(F32)
        for rel in range(3):
            total = total + s2buf[s, c, rel].astype(F32)
        if s == 0:
            hid_loads[c].wait()
        rows = pl.ds(c * BR, BR)
        state = (hown[rows].astype(F32) + total.astype(BF16).astype(F32)).astype(BF16)
        if s == 0:
            hown[rows] = state
        gain = (mgain if s == 0 else fgain)[...].astype(F32)
        mine = block_rows(c, core, chip)
        mfull[s, mine] = normalize(state.astype(F32), gain)
        for rel in range(4):
            gather_copy(s, c, rel, mine).start()

    def forward(s, c):
        for rel in range(3):
            rows = block_rows(c, core, far[rel])
            gather_copy(s, c, rel, rows).wait_recv()
            forward_copy(s, c, rel, rows).start()

    def complete(s, c):
        gather_copy(s, c, 3, block_rows(c, 1 - core, chip)).wait_recv()
        for rel in range(3):
            forward_copy(s, c, rel, block_rows(c, 1 - core, far[rel])).wait_recv()

    def mlp(c):
        if c == 0:
            for copy in loads:
                copy.wait()

        def up(j, carry):
            cols = pl.ds(pl.multiple_of(j * 256, 256), 256)
            values = mfull[0, pl.ds(c * CR, CR)]
            gate = dot(values, wg[:, cols])
            upper = dot(values, wu[:, cols])
            pact[:, cols] = (gate * (1.0 / (1.0 + jnp.exp(-gate))) * upper).astype(BF16)
            return carry

        lax.fori_loop(0, FFN // 256, up, 0)

        def down(which, out):
            rows = pl.ds(pl.multiple_of(which * HALF, HALF), HALF)

            def one(j, carry):
                cols = pl.ds(pl.multiple_of(j * 512, 512), 512)
                out[1, slab(c), cols] = dot(pact[rows], wd[:, cols]).astype(BF16)
                return carry

            lax.fori_loop(0, DIM // 512, one, 0)

        down(1 - core, psib)
        first_copy(1, c).start()
        down(core, pown)

    lane = lax.broadcasted_iota(jnp.int32, (1, 128), 1)

    def absorb(rows, values, weights, col0, valid_last):
        logits = dot(values, weights)
        groups = [logits[:, g * 128:(g + 1) * 128] for g in range(weights.shape[1] // 128)]
        if valid_last is not None:
            groups[-1] = jnp.where(lane < valid_last, groups[-1], -jnp.inf)
        wanted = sid[rows] - (me * VOCAB + col0)
        before = mrun[rows]
        top = before
        for x in groups:
            top = jnp.maximum(top, x)
        total = srun[rows] * jnp.exp(before - top)
        picked = prun[rows]
        for g, x in enumerate(groups):
            total = total + jnp.exp(x - top)
            hit = lane == wanted - g * 128
            if valid_last is not None and g == len(groups) - 1:
                hit = hit & (lane < valid_last)
            picked = picked + jnp.where(hit, x, 0.0)
        mrun[rows] = top
        srun[rows] = total
        prun[rows] = picked

    def vocab(c, events):
        rows = pl.ds(c * CR, CR)

        def step(j, carry):
            t = c * (FULL_TILES + 1) + j

            @pl.when(j + 2 < FULL_TILES)
            def _():
                tile_copy(t + 2, j + 2).start()

            @pl.when(j + 2 == FULL_TILES)
            def _():
                last_copy(t + 2).start()

            if c + 1 < CHUNKS:
                @pl.when(j + 2 > FULL_TILES)
                def _():
                    tile_copy(t + 2, 0).start()

            tile_copy(t, j).wait()
            slot = t % 3
            for n in range(TILE // 256):
                absorb(rows, mfull[1, rows], wbuf[slot, :, n * 256:(n + 1) * 256], j * TILE + n * 256, None)
            return carry

        at = 0
        for stop in sorted(events) + [FULL_TILES]:
            if stop > at:
                lax.fori_loop(at, stop, step, 0)
            at = stop
            for event in events.get(stop, ()):
                event()
        t = c * (FULL_TILES + 1) + FULL_TILES
        if c + 1 < CHUNKS:
            tile_copy(t + 2, 1).start()
        last_copy(t).wait()
        slot = t % 3
        base = FULL_TILES * TILE
        absorb(rows, mfull[1, rows], wbuf[slot, :, 0:256], base, None)
        absorb(rows, mfull[1, rows], wbuf[slot, :, 256:512], base + 256, None)
        tail = jnp.concatenate([wbuf[slot, :, 512:640], wtail[...]], axis=1)
        absorb(rows, mfull[1, rows], tail, base + 512, VOCAB - TAIL_AT)

    project(0)
    project(1)
    pair_sum(0, 0)
    finish_sum(0, 0)
    pair_sum(0, 1)
    forward(0, 0)
    complete(0, 0)
    mlp(0)
    pair_sum(1, 0)
    finish_sum(0, 1)
    finish_sum(1, 0)
    forward(0, 1)
    complete(0, 1)
    mlp(1)
    forward(1, 0)
    complete(1, 0)
    vocab(0, {
        1: (lambda: pair_sum(1, 1),),
        7: (lambda: finish_sum(1, 1),),
        13: (lambda: forward(1, 1),),
    })
    complete(1, 1)
    vocab(1, {})

    for i in range(8):
        rows = pl.ds(i * 128, 128)
        tops = mrun[rows]
        top = jnp.max(tops.T, axis=0, keepdims=True)
        column = jnp.max(tops, axis=1, keepdims=True)
        sums = srun[rows] * jnp.exp(tops - column)
        stat[0, pl.ds(i, 1)] = top
        stat[0, pl.ds(8 + i, 1)] = jnp.sum(sums.T, axis=0, keepdims=True)
        stat[0, pl.ds(16 + i, 1)] = jnp.sum(prun[rows].T, axis=0, keepdims=True)

    def stat_copy(off):
        return remote(stat.at[0], stat.at[off], fin_send.at[off - 1], fin_recv.at[off - 1], (me + off) % 8)

    for off in range(1, 8):
        stat_copy(off).start()
    for off in range(1, 8):
        stat_copy(off).wait_recv()
    top = stat[0, 0:8]
    for off in range(1, 8):
        top = jnp.maximum(top, stat[off, 0:8])
    total = jnp.zeros_like(top)
    picked = jnp.zeros_like(top)
    for off in range(8):
        total = total + stat[off, 8:16] * jnp.exp(stat[off, 0:8] - top)
        picked = picked + stat[off, 16:24]
    log_norm = top + jnp.log(total)
    log_prob = picked - log_norm
    for ref, values in ((ln_ref, log_norm), (lp_ref, log_prob)):
        for i in range(8):
            ref[pl.ds(2 * i, 1), :] = values[i:i + 1, 0:64]
            ref[pl.ds(2 * i + 1, 1), :] = values[i:i + 1, 64:128]

    for s in range(2):
        for c in range(CHUNKS):
            first_copy(s, c).wait_send()
            mine = block_rows(c, core, chip)
            for rel in range(4):
                gather_copy(s, c, rel, mine).wait_send()
            for rel in range(3):
                second_copy(s, c, rel).wait_send()
                forward_copy(s, c, rel, block_rows(c, core, far[rel])).wait_send()
    for off in range(1, 8):
        stat_copy(off).wait_send()


def layer(att, w_o, hidden, mlp_norm, w_gate, w_up, w_down, final_norm, w_lm, w_tail, score_id):
    vmem = pl.BlockSpec(memory_space=pltpu.VMEM)
    hbm = pl.BlockSpec(memory_space=pl.ANY)
    sem = pltpu.SemaphoreType.DMA
    return pl.pallas_call(
        layer_kernel,
        in_specs=[vmem, vmem, hbm, vmem, hbm, hbm, hbm, vmem, hbm, vmem, vmem],
        out_specs=[vmem, vmem],
        out_shape=[jax.ShapeDtypeStruct((16, NODES), F32)] * 2,
        scratch_shapes=[
            pltpu.VMEM((DIM, FFN), BF16),
            pltpu.VMEM((DIM, FFN), BF16),
            pltpu.VMEM((FFN, DIM), BF16),
            pltpu.VMEM((3, DIM, TILE), BF16),
            pltpu.VMEM((2, ROWS // 2, DIM), BF16),
            pltpu.VMEM((2, ROWS // 2, DIM), BF16),
            pltpu.VMEM((2, ROWS // 2, DIM), BF16),
            pltpu.VMEM((2, CHUNKS, 3, BR, DIM), BF16),
            pltpu.VMEM((2, ROWS, DIM), BF16),
            pltpu.VMEM((ROWS // 8, DIM), BF16),
            pltpu.VMEM((CR, FFN), BF16),
            pltpu.VMEM((ROWS, 128), F32),
            pltpu.VMEM((ROWS, 128), F32),
            pltpu.VMEM((ROWS, 128), F32),
            pltpu.VMEM((8, 24, 128), F32),
            sem((3 + CHUNKS,)),
            sem((3,)),
            sem((2, CHUNKS)),
            sem((2, CHUNKS)),
            sem((2, CHUNKS, 3)),
            sem((2, CHUNKS, 3)),
            sem((2, CHUNKS, 4)),
            sem((2, CHUNKS, 4)),
            sem((2, CHUNKS, 3)),
            sem((2, CHUNKS, 3)),
            sem((7,)),
            sem((7,)),
        ],
        compiler_params=pltpu.CompilerParams(collective_id=0, has_side_effects=True, vmem_limit_bytes=63 * 2**20),
        name="layer",
    )(att, w_o, hidden, mlp_norm, w_gate, w_up, w_down, final_norm, w_lm, w_tail, score_id)


def solution(mesh):
    def group_step(hidden, tree_mask, depth, ctx_len, block_table, score_id, k_cache, v_cache, attn_norm, w_q, w_k, w_v, w_o, mlp_norm, w_gate, w_up, w_down, final_norm, w_lm):
        flat = hidden.reshape(ROWS, DIM)
        kv_cache = jnp.concatenate([k_cache[:, :, 0], v_cache[:, :, 0]], axis=-1)
        w_kv = jnp.concatenate([w_k, w_v], axis=1)
        table = jnp.asarray(rope_table())
        att, kv_out = attention(flat, tree_mask, depth[:, None, :], ctx_len, block_table, kv_cache, attn_norm[None], w_q, w_kv, table)
        w_tail = jnp.pad(w_lm[:, TAIL_AT:], ((0, 0), (0, 128 - (VOCAB - TAIL_AT))))
        log_norm, log_prob = layer(att, w_o, flat, mlp_norm[None], w_gate, w_up, w_down, final_norm[None], w_lm, w_tail, score_id.reshape(ROWS, 1))
        return log_norm, log_prob, kv_out[:, :, None, :HD], kv_out[:, :, None, HD:]

    request_spec = P("dp", None, None)
    node_spec = P("dp", None)
    cache_spec = P("dp", None, "tp", None)
    shared_spec = P(None)
    column_spec = P(None, "tp")
    row_spec = P("tp", None)
    in_specs = (request_spec, request_spec, node_spec, P("dp"), node_spec, node_spec, cache_spec, cache_spec, shared_spec, column_spec, column_spec, column_spec, row_spec, shared_spec, column_spec, column_spec, row_spec, shared_spec, column_spec)
    out_specs = (node_spec, node_spec, cache_spec, cache_spec)
    return jax.shard_map(group_step, mesh=mesh, in_specs=in_specs, out_specs=out_specs, check_vma=False)
```

time: 421 us -> 297 us (0.71); the launches traced: 413 us -> 295 us
  Pallas kernels: 0 us -> 197 us
  waiting for transfers between devices: 130 us -> 0 us
  matrix products: 126 us -> 0 us
  blocking collectives: 46.5 us -> 0 us
  local copies, waits for them, and re-layouts: 48.7 us -> 94.9 us
  other arithmetic: 46.8 us -> 1.87 us
  between operations: 15 us -> 0.86 us
    pallas_call x0 -> x2, Pallas kernels: none -> 197 us  [the longest x1 179 us: layer(): pl.pallas_call(layer_kernel, in_specs=[vmem, vmem, hbm, vmem, hbm, hbm, h...]
    psum x2 -> x0, waiting for transfers between devices: 130 us -> none  [the longest x1 72.2 us: layer_and_logits(): lax.psum(jnp.dot(attended, w_o, preferred_element_type=jnp.float32).astyp...]
    dot_general x11 -> x0, matrix products: 126 us -> none  [the longest x1 83.6 us: layer_and_logits(): jnp.dot(rms_norm(layer_out, final_norm), w_lm, preferred_element_type=jnp...]
    unnamed x67 -> x39, local copies, waits for them, and re-layouts: 14.5 us -> 90 us
    reduce_sum x6 -> x0, other arithmetic: 36.5 us -> none  [the longest x1 20.9 us: group_step(): part_sum = jnp.sum(jnp.exp(logits - global_top[..., None]), axis=-1)]
    gather x8 -> x0, local copies, waits for them, and re-layouts: 26.3 us -> none  [the longest x3 16.6 us: group_step(): jnp.take_along_axis(logits, jnp.clip(local_id, 0, vocab_local - 1)[..., N...]
    psum x1 -> x0, blocking collectives: 24.2 us -> none  [group_step(): lax.psum(jnp.stack([part_sum, jnp.where(inside, picked, 0.0)]), 'tp')]
    pmax x1 -> x0, blocking collectives: 22.3 us -> none  [group_step(): global_top = lax.pmax(jnp.max(logits, axis=-1), 'tp')]
  transfers between devices with their start and end apart: 2 -> 0, of which waited for: 2 -> 0; matrix products, arithmetic and copies ran while one was open for 3% -> 0% of each run, Pallas kernels for 0% -> 0%
where the time goes in v1:
time: 297 us; the launch traced here: 295 us
  Pallas kernels  197 us (66%)
  local copies, waits for them, and re-layouts  94.9 us (32%)
    pallas_call x1, Pallas kernels, layer(): pl.pallas_call(layer_kernel, in_specs=[vmem, vmem, hbm, vmem, hbm, hbm, h...  179 us
    unnamed x39, local copies, waits for them, and re-layouts  90 us
    pallas_call x1, Pallas kernels, attention(): pl.pallas_call(functools.partial(attention_kernel, group), grid_spec=spec...  17.9 us

profile of v1, /device:TPU:0, one launch (start us, length us, event | category | flops | bytes accessed | tf_op | source)
XLA Modules:
  0.0 295.0 jit_solution(8914246584476513654)
XLA Ops:
  0.6 0.0 copy-start.8
  0.6 0.0 copy-start.12
  0.7 0.0 copy-start.6
  0.7 0.0 copy-start.7
  0.7 0.0 copy-start.5
  0.7 0.0 copy-start.1
  0.7 1.8 copy.34
  2.5 2.5 copy.35
  5.0 1.6 pad_maximum_fusion.kv_ref
  6.6 0.0 copy-done.8
  6.6 0.3 copy.32
  6.9 1.3 copy.33
  8.2 0.3 pad_maximum_fusion.1.wkv_ref
  8.5 0.0 copy-done.12
  8.5 0.0 copy-done.6
  8.5 0.0 copy-done.7
  8.5 0.0 copy-done.5
  8.5 0.0 copy-done.1
  8.5 0.0 copy-start
  8.5 2.2 copy-done
  10.7 0.0 copy-start.3
  10.7 1.0 copy-done.3
  11.8 0.0 copy-start.4
  11.8 1.0 copy-done.4
  12.7 17.9 %attention.1 = (bf16[1024,256]{1,0:T(8,128)(2,1)S(1)}, bf16[192,16,128]{2,1,0:T(8,128)(2,1)S(1)}) custom-call(s32[16]{0:T(128)S(1)} %copy-done.7, s32[16,12]{1,0:T(8,128)S(1)} %copy-done.5, bf16[1024,2048]{1,0:T(8,128)(2,1)S(1)} %bitcast.9, s32[16,1,64]{2,1,0:T(1,128)S(1)} %bitcast.10, s32[16,64,64]{2,1,0:T(8,128)S(1)} %copy-done.3, ...), custom_call_target="tpu_custom_call" | custom-call | tf_op jit(solution)/shard_map/attention/pallas_call | solution.py:147
  30.7 0.0 copy-start.2
  30.7 0.0 copy-start.9
  30.7 0.0 copy-start.13
  30.7 0.0 copy-start.14
  30.7 75.8 %copy.37.wlm = bf16[2048,16032]{1,0:T(8,128)(2,1)} copy(bf16[2048,16032]{0,1:T(8,128)(2,1)} %param.38) | data formatting | bytes 131334144 | tf_op args[18]
  106.5 0.0 copy-done.2
  106.5 1.1 slice.12
  107.6 0.9 pad.4.wtail
  108.5 0.0 copy-done.9
  108.5 1.3 reshape.16.sid
  109.8 0.0 copy-done.13
  109.8 0.6 broadcast_in_dim.20.mgain
  110.4 0.0 copy-done.14
  110.4 0.6 broadcast_in_dim.21.fgain
  111.0 179.4 %layer.1 = (f32[16,64]{1,0:T(8,128)}, f32[16,64]{1,0:T(8,128)}) custom-call(bf16[1024,256]{1,0:T(8,128)(2,1)} %copy-done.2, bf16[256,2048]{1,0:T(8,128)(2,1)} %wo.1, bf16[1024,2048]{1,0:T(8,128)(2,1)} %bitcast.8, bf16[1,2048]{1,0:T(2,128)(2,1)} %broadcast_in_dim.20.mgain, bf16[2048,1024]{1,0:T(8,128)(2,1)} %wg_hbm.1, bf16[2048,1024]{1,0:T(8,128)(2,1)} %wu_hbm.1, ...), custom_call_target="tpu_custom_call" | custom-call | tf_op jit(solution)/shard_map/layer/pallas_call | solution.py:440
  290.5 0.0 copy-start.11
  290.5 0.0 copy-start.10
  290.5 0.4 slice_bitcast_fusion
  290.9 1.5 copy.39
  292.3 1.5 copy.40
  293.8 0.0 copy-done.11
  293.8 0.6 copy.43
  294.4 0.0 copy-done.10
  294.4 0.6 copy.44
  (1 shorter events, 0.0 us)
Async XLA Ops:
  0.6 6.0 %copy-start.8 = (bf16[2048,64]{0,1:T(8,128)(2,1)S(1)}, bf16[2048,64]{0,1:T(8,128)(2,1)}, u32[]{:S(2)}) copy-start(bf16[2048,64]{0,1:T(8,128)(2,1)} %param.30) | copy-start | bytes 786436
  0.6 7.8 %copy-start.12 = (bf16[2048]{0:T(1024)(128)(2,1)S(1)}, bf16[2048]{0:T(1024)(128)(2,1)}, u32[]{:S(2)}) copy-start(bf16[2048]{0:T(1024)(128)(2,1)} %param.28) | copy-start | bytes 12292
  0.7 7.8 %copy-start.6 = (s32[16,64]{1,0:T(8,128)S(1)}, s32[16,64]{1,0:T(8,128)}, u32[]{:S(2)}) copy-start(s32[16,64]{1,0:T(8,128)} %param.22) | copy-start | bytes 12292
  0.7 7.8 %copy-start.7 = (s32[16]{0:T(128)S(1)}, s32[16]{0:T(128)}, u32[]{:S(2)}) copy-start(s32[16]{0:T(128)} %ctx_ref.1) | copy-start | bytes 196
  0.7 7.8 %copy-start.5 = (s32[16,12]{1,0:T(8,128)S(1)}, s32[16,12]{1,0:T(8,128)}, u32[]{:S(2)}) copy-start(s32[16,12]{1,0:T(8,128)} %bt_ref.1) | copy-start | bytes 2308
  0.7 7.8 %copy-start.1 = (bf16[2048,256]{1,0:T(8,128)(2,1)S(1)}, bf16[2048,256]{1,0:T(8,128)(2,1)}, u32[]{:S(2)}) copy-start(bf16[2048,256]{1,0:T(8,128)(2,1)} %wq_ref.1) | copy-start | bytes 3145732
  8.5 2.2 copy-start
  10.7 1.0 copy-start.3
  11.8 1.0 copy-start.4
  30.7 75.8 %copy-start.2 = (bf16[1024,256]{1,0:T(8,128)(2,1)}, bf16[1024,256]{1,0:T(8,128)(2,1)S(1)}, u32[]{:S(2)}) copy-start(bf16[1024,256]{1,0:T(8,128)(2,1)S(1)} %get-tuple-element.8.att) | copy-start | bytes 1572868
  30.7 77.8 %copy-start.9 = (s32[16,64]{1,0:T(8,128)S(1)}, s32[16,64]{1,0:T(8,128)}, u32[]{:S(2)}) copy-start(s32[16,64]{1,0:T(8,128)} %param.25) | copy-start | bytes 12292
  30.7 79.1 %copy-start.13 = (bf16[2048]{0:T(1024)(128)(2,1)S(1)}, bf16[2048]{0:T(1024)(128)(2,1)}, u32[]{:S(2)}) copy-start(bf16[2048]{0:T(1024)(128)(2,1)} %param.33) | copy-start | bytes 12292
  30.7 79.7 %copy-start.14 = (bf16[2048]{0:T(1024)(128)(2,1)S(1)}, bf16[2048]{0:T(1024)(128)(2,1)}, u32[]{:S(2)}) copy-start(bf16[2048]{0:T(1024)(128)(2,1)} %param.37) | copy-start | bytes 12292
  290.5 3.3 %copy-start.11 = (f32[16,64]{1,0:T(8,128)S(1)}, f32[16,64]{1,0:T(8,128)}, u32[]{:S(2)}) copy-start(f32[16,64]{1,0:T(8,128)} %get-tuple-element.26) | copy-start | bytes 12292
  290.5 3.9 %copy-start.10 = (f32[16,64]{1,0:T(8,128)S(1)}, f32[16,64]{1,0:T(8,128)}, u32[]{:S(2)}) copy-start(f32[16,64]{1,0:T(8,128)} %get-tuple-element.27) | copy-start | bytes 12292

commit v2 on v1

--- a/solution.py
+++ b/solution.py
@@ -19,10 +19,10 @@
 HD = 64
 FFN = 1024
 VOCAB = 16032
-TILE = 1024
-FULL_TILES = 15
-LAST = 640
-TAIL_AT = 16000
+TILE = 1008
+TILES = 16
+REPEAT = TILES * TILE - VOCAB
+LOWEST = -3e38
 CHUNKS = 2
 CR = ROWS // CHUNKS
 HALF = CR // 2
@@ -64,11 +64,11 @@
     return lax.dot_general(a, b, (((0,), (0,)), ((), ())), preferred_element_type=F32)
 
 
-def attention_kernel(group, ctx_ref, bt_ref, hid_ref, depth_ref, mask_ref, gain_ref, wq_ref, wkv_ref, table_ref, kv_ref, att_ref, kvout_ref, old_ref):
+def attention_kernel(group, ctx_ref, bt_ref, hid_ref, depth_ref, mask_ref, gain_ref, wq_ref, wk_ref, wv_ref, table_ref, kv_ref, att_ref, kvout_ref, old_ref):
     step = pl.program_id(0)
     normed = normalize(hid_ref[...].astype(F32), gain_ref[...].astype(F32))
     q_all = dot(normed, wq_ref[...])
-    kv_all = dot(normed, wkv_ref[...])
+    kv_all = dot_nt(normed, jnp.concatenate([wk_ref[...], wv_ref[...]], axis=0))
     lane = lax.broadcasted_iota(jnp.int32, (1, 128), 1)
     low = lane < 64
     first = (lane % 64) < 32
@@ -122,7 +122,7 @@
             att_ref[rows, pair * 128:(pair + 1) * 128] = (mixed / jnp.where(low, t_even, t_odd)).astype(BF16)
 
 
-def attention(hidden, tree_mask, depth, ctx_len, block_table, kv_cache, attn_norm, w_q, w_kv, table):
+def attention(hidden, tree_mask, depth, ctx_len, block_table, kv_cache, attn_norm, w_q, w_k, w_v, table):
     group = 4
     grid = (hidden.shape[0] // (group * NODES),)
     spec = pltpu.PrefetchScalarGridSpec(
@@ -134,7 +134,8 @@
             pl.BlockSpec((group, NODES, NODES), lambda i, *_: (i, 0, 0)),
             pl.BlockSpec((1, DIM), lambda i, *_: (0, 0)),
             pl.BlockSpec((DIM, 256), lambda i, *_: (0, 0)),
-            pl.BlockSpec((DIM, 128), lambda i, *_: (0, 0)),
+            pl.BlockSpec((HD, DIM), lambda i, *_: (0, 0)),
+            pl.BlockSpec((HD, DIM), lambda i, *_: (0, 0)),
             pl.BlockSpec(table.shape, lambda i, *_: (0, 0)),
             pl.BlockSpec(kv_cache.shape, lambda i, *_: (0, 0, 0)),
         ],
@@ -150,11 +151,11 @@
         out_shape=[jax.ShapeDtypeStruct((hidden.shape[0], 256), BF16), jax.ShapeDtypeStruct(kv_cache.shape, BF16)],
         compiler_params=pltpu.CompilerParams(vmem_limit_bytes=40 * 2**20),
         name="attention",
-    )(ctx_len, block_table, hidden, depth, tree_mask, attn_norm, w_q, w_kv, table, kv_cache)
-
-
-def layer_kernel(att, wo, hid, mgain, wg_hbm, wu_hbm, wd_hbm, fgain, wlm, wtail, sid, ln_ref, lp_ref,
-                 wg, wu, wd, wbuf, psib, pown, s1buf, s2buf, mfull, hown, pact, mrun, srun, prun, stat,
+    )(ctx_len, block_table, hidden, depth, tree_mask, attn_norm, w_q, w_k, w_v, table, kv_cache)
+
+
+def layer_kernel(att, wo, hid, mgain, wg_hbm, wu_hbm, wd_hbm, fgain, wlm, sid, ln_ref, lp_ref,
+                 wg, wu, wd, wbuf, psib, pown, s1buf, s2buf, mfull, hown, pact, lg0, lg1, mrun, srun, prun, wanted, stat,
                  load_sem, tile_sem, s1_send, s1_recv, s2_send, s2_recv, ag_send, ag_recv, fw_send, fw_recv, fin_send, fin_recv):
     me = lax.axis_index("tp")
     core = me % 2
@@ -190,18 +191,18 @@
     for copy in hid_loads + loads:
         copy.start()
 
-    def tile_copy(t, j):
-        return pltpu.make_async_copy(wlm.at[:, pl.ds(pl.multiple_of(j * TILE, TILE), TILE)], wbuf.at[t % 3], tile_sem.at[t % 3])
-
-    def last_copy(t):
-        return pltpu.make_async_copy(wlm.at[:, pl.ds(FULL_TILES * TILE, LAST)], wbuf.at[t % 3, :, pl.ds(0, LAST)], tile_sem.at[t % 3])
-
-    tile_copy(0, 0).start()
-    tile_copy(1, 1).start()
-
-    mrun[...] = jnp.full_like(mrun, -jnp.inf)
+    def tile_copy(t):
+        first = jnp.minimum((t % TILES) * TILE, VOCAB - TILE)
+        return pltpu.make_async_copy(wlm.at[pl.ds(pl.multiple_of(first, 16), TILE)], wbuf.at[t % 4], tile_sem.at[t % 4])
+
+    tile_copy(0).start()
+    tile_copy(1).start()
+
+    mrun[...] = jnp.full_like(mrun, LOWEST)
     srun[...] = jnp.zeros_like(srun)
     prun[...] = jnp.zeros_like(prun)
+    for i in range(16):
+        wanted[:, pl.ds(i * NODES, NODES)] = sid[pl.ds(i, 1)] - me * VOCAB
 
     def half_rows(c, which):
         return pl.ds(pl.multiple_of(c * CR + which * HALF, HALF), HALF)
@@ -297,72 +298,63 @@
         first_copy(1, c).start()
         down(core, pown)
 
-    lane = lax.broadcasted_iota(jnp.int32, (1, 128), 1)
-
-    def absorb(rows, values, weights, col0, valid_last):
-        logits = dot(values, weights)
-        groups = [logits[:, g * 128:(g + 1) * 128] for g in range(weights.shape[1] // 128)]
-        if valid_last is not None:
-            groups[-1] = jnp.where(lane < valid_last, groups[-1], -jnp.inf)
-        wanted = sid[rows] - (me * VOCAB + col0)
-        before = mrun[rows]
-        top = before
-        for x in groups:
-            top = jnp.maximum(top, x)
-        total = srun[rows] * jnp.exp(before - top)
-        picked = prun[rows]
-        for g, x in enumerate(groups):
-            total = total + jnp.exp(x - top)
-            hit = lane == wanted - g * 128
-            if valid_last is not None and g == len(groups) - 1:
-                hit = hit & (lane < valid_last)
-            picked = picked + jnp.where(hit, x, 0.0)
-        mrun[rows] = top
-        srun[rows] = total
-        prun[rows] = picked
-
-    def vocab(c, events):
-        rows = pl.ds(c * CR, CR)
-
-        def step(j, carry):
-            t = c * (FULL_TILES + 1) + j
-
-            @pl.when(j + 2 < FULL_TILES)
+    def chunk_rows(t):
+        return pl.ds(pl.multiple_of((t // TILES) * CR, CR), CR)
+
+    def multiply(logits, t):
+        logits[...] = dot_nt(wbuf[t % 4], mfull[1, chunk_rows(t)])
+
+    def absorb(logits, t):
+        j = (t + TILES) % TILES
+        rows = chunk_rows(jnp.maximum(t, 0))
+        last = j == TILES - 1
+        blocks = []
+        for g in range(TILE // 8):
+            x = logits[g * 8:(g + 1) * 8, :]
+            blocks.append(jnp.where(last, -jnp.inf, x) if g * 8 < REPEAT else x)
+        first = jnp.where(t < 0, 2 * VOCAB * 8, jnp.minimum(j * TILE, VOCAB - TILE))
+        offset = wanted[:, rows] - first - lax.broadcasted_iota(jnp.int32, (8, CR), 0)
+        before = mrun[:, rows]
+        tops = [before] + [None] * 3
+        for g, x in enumerate(blocks):
+            old = tops[g % 4]
+            tops[g % 4] = x if old is None else jnp.maximum(old, x)
+        top = jnp.maximum(jnp.maximum(tops[0], tops[1]), jnp.maximum(tops[2], tops[3]))
+        totals = [srun[:, rows] * jnp.exp(before - top)] + [jnp.zeros_like(top)] * 3
+        picked = [prun[:, rows]] + [jnp.zeros_like(top)] * 3
+        for g, x in enumerate(blocks):
+            totals[g % 4] = totals[g % 4] + jnp.exp(x - top)
+            hit = offset == g * 8
+            if g * 8 < REPEAT:
+                hit = hit & jnp.logical_not(last)
+            picked[g % 4] = picked[g % 4] + jnp.where(hit, x, 0.0)
+        mrun[:, rows] = top
+        srun[:, rows] = (totals[0] + totals[1]) + (totals[2] + totals[3])
+        prun[:, rows] = (picked[0] + picked[1]) + (picked[2] + picked[3])
+
+    def vocab(events):
+        lg1[...] = jnp.full_like(lg1, LOWEST)
+
+        def step(i, carry):
+            t = 2 * i
+
+            @pl.when(t + 2 < CHUNKS * TILES)
             def _():
-                tile_copy(t + 2, j + 2).start()
-
-            @pl.when(j + 2 == FULL_TILES)
-            def _():
-                last_copy(t + 2).start()
-
-            if c + 1 < CHUNKS:
-                @pl.when(j + 2 > FULL_TILES)
-                def _():
-                    tile_copy(t + 2, 0).start()
-
-            tile_copy(t, j).wait()
-            slot = t % 3
-            for n in range(TILE // 256):
-                absorb(rows, mfull[1, rows], wbuf[slot, :, n * 256:(n + 1) * 256], j * TILE + n * 256, None)
+                tile_copy(t + 2).start()
+                tile_copy(t + 3).start()
+
+            for at, event in events:
+                pl.when(i == at)(event)
+            tile_copy(t).wait()
+            tile_copy(t + 1).wait()
+            multiply(lg0, t)
+            absorb(lg1, t - 1)
+            multiply(lg1, t + 1)
+            absorb(lg0, t)
             return carry
 
-        at = 0
-        for stop in sorted(events) + [FULL_TILES]:
-            if stop > at:
-                lax.fori_loop(at, stop, step, 0)
-            at = stop
-            for event in events.get(stop, ()):
-                event()
-        t = c * (FULL_TILES + 1) + FULL_TILES
-        if c + 1 < CHUNKS:
-            tile_copy(t + 2, 1).start()
-        last_copy(t).wait()
-        slot = t % 3
-        base = FULL_TILES * TILE
-        absorb(rows, mfull[1, rows], wbuf[slot, :, 0:256], base, None)
-        absorb(rows, mfull[1, rows], wbuf[slot, :, 256:512], base + 256, None)
-        tail = jnp.concatenate([wbuf[slot, :, 512:640], wtail[...]], axis=1)
-        absorb(rows, mfull[1, rows], tail, base + 512, VOCAB - TAIL_AT)
+        lax.fori_loop(0, CHUNKS * TILES // 2, step, 0)
+        absorb(lg1, CHUNKS * TILES - 1)
 
     project(0)
     project(1)
@@ -380,23 +372,18 @@
     mlp(1)
     forward(1, 0)
     complete(1, 0)
-    vocab(0, {
-        1: (lambda: pair_sum(1, 1),),
-        7: (lambda: finish_sum(1, 1),),
-        13: (lambda: forward(1, 1),),
-    })
-    complete(1, 1)
-    vocab(1, {})
-
-    for i in range(8):
-        rows = pl.ds(i * 128, 128)
-        tops = mrun[rows]
-        top = jnp.max(tops.T, axis=0, keepdims=True)
-        column = jnp.max(tops, axis=1, keepdims=True)
-        sums = srun[rows] * jnp.exp(tops - column)
-        stat[0, pl.ds(i, 1)] = top
-        stat[0, pl.ds(8 + i, 1)] = jnp.sum(sums.T, axis=0, keepdims=True)
-        stat[0, pl.ds(16 + i, 1)] = jnp.sum(prun[rows].T, axis=0, keepdims=True)
+    vocab((
+        (1, lambda: pair_sum(1, 1)),
+        (4, lambda: finish_sum(1, 1)),
+        (7, lambda: forward(1, 1)),
+        (8, lambda: complete(1, 1)),
+    ))
+
+    tops = mrun[...]
+    top = jnp.max(tops, axis=0, keepdims=True)
+    stat[0, 0:1] = top
+    stat[0, 1:2] = jnp.sum(srun[...] * jnp.exp(tops - top), axis=0, keepdims=True)
+    stat[0, 2:3] = jnp.sum(prun[...], axis=0, keepdims=True)
 
     def stat_copy(off):
         return remote(stat.at[0], stat.at[off], fin_send.at[off - 1], fin_recv.at[off - 1], (me + off) % 8)
@@ -405,20 +392,19 @@
         stat_copy(off).start()
     for off in range(1, 8):
         stat_copy(off).wait_recv()
-    top = stat[0, 0:8]
+    top = stat[0, 0:1]
     for off in range(1, 8):
-        top = jnp.maximum(top, stat[off, 0:8])
+        top = jnp.maximum(top, stat[off, 0:1])
     total = jnp.zeros_like(top)
     picked = jnp.zeros_like(top)
     for off in range(8):
-        total = total + stat[off, 8:16] * jnp.exp(stat[off, 0:8] - top)
-        picked = picked + stat[off, 16:24]
+        total = total + stat[off, 1:2] * jnp.exp(stat[off, 0:1] - top)
+        picked = picked + stat[off, 2:3]
     log_norm = top + jnp.log(total)
     log_prob = picked - log_norm
-    for ref, values in ((ln_ref, log_norm), (lp_ref, log_prob)):
-        for i in range(8):
-            ref[pl.ds(2 * i, 1), :] = values[i:i + 1, 0:64]
-            ref[pl.ds(2 * i + 1, 1), :] = values[i:i + 1, 64:128]
+    for i in range(16):
+        ln_ref[pl.ds(i, 1), :] = log_norm[:, i * NODES:(i + 1) * NODES]
+        lp_ref[pl.ds(i, 1), :] = log_prob[:, i * NODES:(i + 1) * NODES]
 
     for s in range(2):
         for c in range(CHUNKS):
@@ -433,20 +419,20 @@
         stat_copy(off).wait_send()
 
 
-def layer(att, w_o, hidden, mlp_norm, w_gate, w_up, w_down, final_norm, w_lm, w_tail, score_id):
+def layer(att, w_o, hidden, mlp_norm, w_gate, w_up, w_down, final_norm, w_lm, score_id):
     vmem = pl.BlockSpec(memory_space=pltpu.VMEM)
     hbm = pl.BlockSpec(memory_space=pl.ANY)
     sem = pltpu.SemaphoreType.DMA
     return pl.pallas_call(
         layer_kernel,
-        in_specs=[vmem, vmem, hbm, vmem, hbm, hbm, hbm, vmem, hbm, vmem, vmem],
+        in_specs=[vmem, vmem, hbm, vmem, hbm, hbm, hbm, vmem, hbm, vmem],
         out_specs=[vmem, vmem],
         out_shape=[jax.ShapeDtypeStruct((16, NODES), F32)] * 2,
         scratch_shapes=[
             pltpu.VMEM((DIM, FFN), BF16),
             pltpu.VMEM((DIM, FFN), BF16),
             pltpu.VMEM((FFN, DIM), BF16),
-            pltpu.VMEM((3, DIM, TILE), BF16),
+            pltpu.VMEM((4, TILE, DIM), BF16),
             pltpu.VMEM((2, ROWS // 2, DIM), BF16),
             pltpu.VMEM((2, ROWS // 2, DIM), BF16),
             pltpu.VMEM((2, ROWS // 2, DIM), BF16),
@@ -454,12 +440,15 @@
             pltpu.VMEM((2, ROWS, DIM), BF16),
             pltpu.VMEM((ROWS // 8, DIM), BF16),
             pltpu.VMEM((CR, FFN), BF16),
-            pltpu.VMEM((ROWS, 128), F32),
-            pltpu.VMEM((ROWS, 128), F32),
-            pltpu.VMEM((ROWS, 128), F32),
-            pltpu.VMEM((8, 24, 128), F32),
+            pltpu.VMEM((TILE, CR), F32),
+            pltpu.VMEM((TILE, CR), F32),
+            pltpu.VMEM((8, ROWS), F32),
+            pltpu.VMEM((8, ROWS), F32),
+            pltpu.VMEM((8, ROWS), F32),
+            pltpu.VMEM((1, ROWS), jnp.int32),
+            pltpu.VMEM((8, 8, ROWS), F32),
             sem((3 + CHUNKS,)),
-            sem((3,)),
+            sem((4,)),
             sem((2, CHUNKS)),
             sem((2, CHUNKS)),
             sem((2, CHUNKS, 3)),
@@ -473,18 +462,16 @@
         ],
         compiler_params=pltpu.CompilerParams(collective_id=0, has_side_effects=True, vmem_limit_bytes=63 * 2**20),
         name="layer",
-    )(att, w_o, hidden, mlp_norm, w_gate, w_up, w_down, final_norm, w_lm, w_tail, score_id)
+    )(att, w_o, hidden, mlp_norm, w_gate, w_up, w_down, final_norm, w_lm, score_id)
 
 
 def solution(mesh):
     def group_step(hidden, tree_mask, depth, ctx_len, block_table, score_id, k_cache, v_cache, attn_norm, w_q, w_k, w_v, w_o, mlp_norm, w_gate, w_up, w_down, final_norm, w_lm):
         flat = hidden.reshape(ROWS, DIM)
         kv_cache = jnp.concatenate([k_cache[:, :, 0], v_cache[:, :, 0]], axis=-1)
-        w_kv = jnp.concatenate([w_k, w_v], axis=1)
         table = jnp.asarray(rope_table())
-        att, kv_out = attention(flat, tree_mask, depth[:, None, :], ctx_len, block_table, kv_cache, attn_norm[None], w_q, w_kv, table)
-        w_tail = jnp.pad(w_lm[:, TAIL_AT:], ((0, 0), (0, 128 - (VOCAB - TAIL_AT))))
-        log_norm, log_prob = layer(att, w_o, flat, mlp_norm[None], w_gate, w_up, w_down, final_norm[None], w_lm, w_tail, score_id.reshape(ROWS, 1))
+        att, kv_out = attention(flat, tree_mask, depth[:, None, :], ctx_len, block_table, kv_cache, attn_norm[None], w_q, w_k.T, w_v.T, table)
+        log_norm, log_prob = layer(att, w_o, flat, mlp_norm[None], w_gate, w_up, w_down, final_norm[None], w_lm.T, score_id)
         return log_norm, log_prob, kv_out[:, :, None, :HD], kv_out[:, :, None, HD:]
 
     request_spec = P("dp", None, None)

time: 297 us -> 212 us (0.71)
  local copies, waits for them, and re-layouts: 94.9 us -> 13.1 us
    unnamed x39 -> x36, local copies, waits for them, and re-layouts: 90 us -> 11.5 us
where the time goes in v2:
time: 212 us
  Pallas kernels  196 us (92%)
  local copies, waits for them, and re-layouts  13.1 us (6%)
    pallas_call x1, Pallas kernels, layer(): pl.pallas_call(layer_kernel, in_specs=[vmem, vmem, hbm, vmem, hbm, hbm, h...  179 us
    pallas_call x1, Pallas kernels, attention(): pl.pallas_call(functools.partial(attention_kernel, group), grid_spec=spec...  17.6 us
    unnamed x36, local copies, waits for them, and re-layouts  11.5 us

profile of v2, /device:TPU:0, one launch (start us, length us, event | category | flops | bytes accessed | tf_op | source)
XLA Modules:
  0.0 211.8 jit_solution(12323107490290086960)
XLA Ops:
  0.6 0.0 copy-start.4
  0.6 0.0 copy-start.12
  0.7 0.0 copy-start.8
  0.7 0.0 copy-start.5
  0.7 0.0 copy-start.6
  0.7 0.0 copy-start.3
  0.7 0.0 copy-start.9
  0.7 0.0 copy-start.7
  0.7 0.0 copy-start.1
  0.7 1.8 copy.24
  2.6 2.5 %copy.25 = bf16[192,16,1,64]{3,1,0,2:T(8,128)(2,1)} copy(bf16[192,16,1,64]{0,3,2,1:T(8,128)(2,1)} %param.27) | data formatting | bytes 786432 | tf_op args[7]
  5.1 1.6 pad_maximum_fusion.kv_ref
  6.7 0.0 copy-done.12
  6.7 0.0 copy-start.13
  6.7 0.0 copy-start.14
  6.7 0.0 copy-done.4
  6.7 0.0 copy-done.8
  6.8 0.0 copy-done.5
  6.8 0.0 copy-done.6
  6.8 0.0 copy-done.3
  6.8 0.0 copy-done.9
  6.8 0.0 copy-done.7
  6.8 0.0 copy-done.1
  6.8 0.0 copy-start
  6.8 2.2 %copy-done = bf16[16,64,2048]{2,1,0:T(8,128)(2,1)S(1)} copy-done((bf16[16,64,2048]{2,1,0:T(8,128)(2,1)S(1)}, bf16[16,64,2048]{2,1,0:T(8,128)(2,1)}, u32[]{:S(2)}) %copy-start) | copy-done | bytes 4194328
  9.0 17.6 %attention.1 = (bf16[1024,256]{1,0:T(8,128)(2,1)S(1)}, bf16[192,16,128]{2,1,0:T(8,128)(2,1)S(1)}) custom-call(s32[16]{0:T(128)S(1)} %copy-done.9, s32[16,12]{1,0:T(8,128)S(1)} %copy-done.7, bf16[1024,2048]{1,0:T(8,128)(2,1)S(1)} %bitcast.12, s32[16,1,64]{2,1,0:T(1,128)S(1)} %bitcast.15, s32[16,64,64]{2,1,0:T(8,128)S(1)} %copy-done.3, ...), custom_call_target="tpu_custom_call" | custom-call | tf_op jit(solution)/shard_map/attention/pallas_call | solution.py:148
  26.6 0.0 copy-start.2
  26.7 0.8 copy-done.2
  27.4 0.0 copy-done.13
  27.4 0.6 broadcast_in_dim.20.mgain
  28.1 0.0 copy-done.14
  28.1 0.6 broadcast_in_dim.21.fgain
  28.7 178.6 %layer.1 = (f32[16,64]{1,0:T(8,128)}, f32[16,64]{1,0:T(8,128)}) custom-call(bf16[1024,256]{1,0:T(8,128)(2,1)} %copy-done.2, bf16[256,2048]{1,0:T(8,128)(2,1)} %wo.1, bf16[1024,2048]{1,0:T(8,128)(2,1)} %bitcast.11, bf16[1,2048]{1,0:T(2,128)(2,1)} %broadcast_in_dim.20.mgain, bf16[2048,1024]{1,0:T(8,128)(2,1)} %wg_hbm.1, bf16[2048,1024]{1,0:T(8,128)(2,1)} %wu_hbm.1, ...), custom_call_target="tpu_custom_call" | custom-call | tf_op jit(solution)/shard_map/layer/pallas_call | solution.py:426
  207.3 0.0 copy-start.11
  207.3 0.0 copy-start.10
  207.3 0.4 slice_bitcast_fusion
  207.7 1.5 copy.26
  209.1 1.5 copy.27
  210.6 0.0 copy-done.11
  210.6 0.6 copy.30
  211.2 0.0 copy-done.10
  211.2 0.6 copy.31
  (1 shorter events, 0.0 us)
Async XLA Ops:
  0.6 6.1 %copy-start.4 = (bf16[192,768]{1,0:T(8,128)(2,1)S(1)}, bf16[192,768]{1,0:T(8,128)(2,1)}, u32[]{:S(2)}) copy-start(bf16[192,768]{1,0:T(8,128)(2,1)} %constant.2.clone.table_ref) | copy-start | bytes 884740
  0.6 6.0 %copy-start.12 = (bf16[2048]{0:T(1024)(128)(2,1)S(1)}, bf16[2048]{0:T(1024)(128)(2,1)}, u32[]{:S(2)}) copy-start(bf16[2048]{0:T(1024)(128)(2,1)} %param.28) | copy-start | bytes 12292
  0.7 6.1 %copy-start.8 = (s32[16,64]{1,0:T(8,128)S(1)}, s32[16,64]{1,0:T(8,128)}, u32[]{:S(2)}) copy-start(s32[16,64]{1,0:T(8,128)} %param.22) | copy-start | bytes 12292
  0.7 6.1 %copy-start.5 = (bf16[2048,64]{0,1:T(8,128)(2,1)S(1)}, bf16[2048,64]{0,1:T(8,128)(2,1)}, u32[]{:S(2)}) copy-start(bf16[2048,64]{0,1:T(8,128)(2,1)} %param.30) | copy-start | bytes 786436
  0.7 6.1 %copy-start.6 = (bf16[2048,64]{0,1:T(8,128)(2,1)S(1)}, bf16[2048,64]{0,1:T(8,128)(2,1)}, u32[]{:S(2)}) copy-start(bf16[2048,64]{0,1:T(8,128)(2,1)} %param.31) | copy-start | bytes 786436
  0.7 6.1 %copy-start.3 = (s32[16,64,64]{2,1,0:T(8,128)S(1)}, s32[16,64,64]{2,1,0:T(8,128)}, u32[]{:S(2)}) copy-start(s32[16,64,64]{2,1,0:T(8,128)} %mask_ref.1) | copy-start | bytes 786436
  0.7 6.1 %copy-start.9 = (s32[16]{0:T(128)S(1)}, s32[16]{0:T(128)}, u32[]{:S(2)}) copy-start(s32[16]{0:T(128)} %ctx_ref.1) | copy-start | bytes 196
  0.7 6.1 %copy-start.7 = (s32[16,12]{1,0:T(8,128)S(1)}, s32[16,12]{1,0:T(8,128)}, u32[]{:S(2)}) copy-start(s32[16,12]{1,0:T(8,128)} %bt_ref.1) | copy-start | bytes 2308
  0.7 6.1 %copy-start.1 = (bf16[2048,256]{1,0:T(8,128)(2,1)S(1)}, bf16[2048,256]{1,0:T(8,128)(2,1)}, u32[]{:S(2)}) copy-start(bf16[2048,256]{1,0:T(8,128)(2,1)} %wq_ref.1) | copy-start | bytes 3145732
  6.7 20.8 %copy-start.13 = (bf16[2048]{0:T(1024)(128)(2,1)S(1)}, bf16[2048]{0:T(1024)(128)(2,1)}, u32[]{:S(2)}) copy-start(bf16[2048]{0:T(1024)(128)(2,1)} %param.33) | copy-start | bytes 12292
  6.7 21.3 %copy-start.14 = (bf16[2048]{0:T(1024)(128)(2,1)S(1)}, bf16[2048]{0:T(1024)(128)(2,1)}, u32[]{:S(2)}) copy-start(bf16[2048]{0:T(1024)(128)(2,1)} %param.37) | copy-start | bytes 12292
  6.8 2.2 %copy-start = (bf16[16,64,2048]{2,1,0:T(8,128)(2,1)S(1)}, bf16[16,64,2048]{2,1,0:T(8,128)(2,1)}, u32[]{:S(2)}) copy-start(bf16[16,64,2048]{2,1,0:T(8,128)(2,1)} %param.20) | copy-start | bytes 12582916
  26.6 0.8 copy-start.2
  207.3 3.3 %copy-start.11 = (f32[16,64]{1,0:T(8,128)S(1)}, f32[16,64]{1,0:T(8,128)}, u32[]{:S(2)}) copy-start(f32[16,64]{1,0:T(8,128)} %get-tuple-element.22) | copy-start | bytes 12292
  207.3 3.9 %copy-start.10 = (f32[16,64]{1,0:T(8,128)S(1)}, f32[16,64]{1,0:T(8,128)}, u32[]{:S(2)}) copy-start(f32[16,64]{1,0:T(8,128)} %get-tuple-element.23) | copy-start | bytes 12292

commit v3 on v2

--- a/solution.py
+++ b/solution.py
@@ -23,13 +23,20 @@
 TILES = 16
 REPEAT = TILES * TILE - VOCAB
 LOWEST = -3e38
-CHUNKS = 2
+CHUNKS = 4
+PASSES = 2
+PR = ROWS // PASSES
+HD_COLS = DIM // 2
 CR = ROWS // CHUNKS
 HALF = CR // 2
 BR = CR // 8
 MESH = pl.DeviceIdType.MESH
 F32 = jnp.float32
 BF16 = jnp.bfloat16
+
+
+BEFORE = "O0 O1 A00 A01 R00 R01 B00 B01 O2 O3 F00 A02 F01 C00 M0 C01 A10 M1 A11 R02 R10 B10 R11 B11 F10 F11 C10 C11"
+DURING = ("B02 A03", "R03 F02", "B03 C02 M2", "F03 A12 C03 M3", "R12 A13", "B12 R13", "B13 F12", "C12 F13", "C13")
 
 
 def rope_table():
@@ -156,7 +163,7 @@
 
 def layer_kernel(att, wo, hid, mgain, wg_hbm, wu_hbm, wd_hbm, fgain, wlm, sid, ln_ref, lp_ref,
                  wg, wu, wd, wbuf, psib, pown, s1buf, s2buf, mfull, hown, pact, lg0, lg1, mrun, srun, prun, wanted, stat,
-                 load_sem, tile_sem, s1_send, s1_recv, s2_send, s2_recv, ag_send, ag_recv, fw_send, fw_recv, fin_send, fin_recv):
+                 load_sem, tile_sem, s1_send, s1_recv, s2_send, s2_recv, ag_send, ag_recv, fw_send, fw_recv, cr_send, cr_recv, fin_send, fin_recv):
     me = lax.axis_index("tp")
     core = me % 2
     chip = me // 2
@@ -220,15 +227,31 @@
         first_copy(0, c).start()
         pown[0, slab(c)] = dot(att[half_rows(c, core)], wo[...]).astype(BF16)
 
-    def second_copy(s, c, rel):
-        block = pl.ds(pl.multiple_of(c * HALF + far[rel] * BR, BR), BR)
-        return remote(pown.at[s, block], s2buf.at[s, c, rel], s2_send.at[s, c, rel], s2_recv.at[s, c, rel], peer(rel))
+    first_cols = pl.ds(0, HD_COLS)
+    last_cols = pl.ds(HD_COLS, HD_COLS)
+
+    def stored(c, q):
+        return pl.ds(pl.multiple_of(c * HALF + q * BR, BR), BR)
+
+    def second_copy(s, c, i):
+        q = (far[0], far[2], far[1], far[2], far[1], far[0])[i]
+        target = peer((0, 0, 1, 1, 1, 0)[i])
+        cols = (first_cols, first_cols, last_cols, last_cols, first_cols, last_cols)[i]
+        return remote(pown.at[s, stored(c, q), cols], s2buf.at[s, c, i], s2_send.at[s, c, i], s2_recv.at[s, c, i], target)
 
     def pair_sum(s, c):
         first_copy(s, c).wait_recv()
         pown[s, slab(c)] = (pown[s, slab(c)].astype(F32) + s1buf[s, slab(c)].astype(F32)).astype(BF16)
-        for rel in range(3):
-            second_copy(s, c, rel).start()
+        for i in (1, 3, 0, 2):
+            second_copy(s, c, i).start()
+
+    def relay(s, c):
+        for i, q, cols in ((1, far[1], first_cols), (3, far[0], last_cols)):
+            second_copy(s, c, i).wait_recv()
+            rows = stored(c, q)
+            pown[s, rows, cols] = (pown[s, rows, cols].astype(F32) + s2buf[s, c, i].astype(F32)).astype(BF16)
+        for i in (4, 5):
+            second_copy(s, c, i).start()
 
     def block_rows(c, k, q):
         return pl.ds(pl.multiple_of(c * CR + (k * 4 + q) * BR, BR), BR)
@@ -241,11 +264,12 @@
         return remote(mfull.at[s, rows], mfull.at[s, rows], fw_send.at[s, c, rel], fw_recv.at[s, c, rel], sib)
 
     def finish_sum(s, c):
-        for rel in range(3):
-            second_copy(s, c, rel).wait_recv()
-        total = pown[s, pl.ds(pl.multiple_of(c * HALF + chip * BR, BR), BR)].astype(F32)
-        for rel in range(3):
-            total = total + s2buf[s, c, rel].astype(F32)
+        for i in (0, 2, 4, 5):
+            second_copy(s, c, i).wait_recv()
+        rows = stored(c, chip)
+        left = pown[s, rows, first_cols].astype(F32) + s2buf[s, c, 0].astype(F32) + s2buf[s, c, 4].astype(F32)
+        right = pown[s, rows, last_cols].astype(F32) + s2buf[s, c, 2].astype(F32) + s2buf[s, c, 5].astype(F32)
+        total = jnp.concatenate([left, right], axis=1)
         if s == 0:
             hid_loads[c].wait()
         rows = pl.ds(c * BR, BR)
@@ -255,16 +279,26 @@
         gain = (mgain if s == 0 else fgain)[...].astype(F32)
         mine = block_rows(c, core, chip)
         mfull[s, mine] = normalize(state.astype(F32), gain)
-        for rel in range(4):
+        for rel in (0, 1, 3):
             gather_copy(s, c, rel, mine).start()
 
+    def cross_copy(s, c, i, q):
+        rows = block_rows(c, core, q)
+        cols = (last_cols, first_cols)[i]
+        part = mfull.at[s, rows, cols]
+        return remote(part, part, cr_send.at[s, c, i], cr_recv.at[s, c, i], peer(1 - i))
+
     def forward(s, c):
-        for rel in range(3):
+        for rel in range(2):
             rows = block_rows(c, core, far[rel])
             gather_copy(s, c, rel, rows).wait_recv()
+            cross_copy(s, c, rel, far[rel]).start()
             forward_copy(s, c, rel, rows).start()
 
     def complete(s, c):
+        for i in range(2):
+            cross_copy(s, c, i, far[2]).wait_recv()
+        forward_copy(s, c, 2, block_rows(c, core, far[2])).start()
         gather_copy(s, c, 3, block_rows(c, 1 - core, chip)).wait_recv()
         for rel in range(3):
             forward_copy(s, c, rel, block_rows(c, 1 - core, far[rel])).wait_recv()
@@ -299,10 +333,12 @@
         down(core, pown)
 
     def chunk_rows(t):
-        return pl.ds(pl.multiple_of((t // TILES) * CR, CR), CR)
+        return pl.ds(pl.multiple_of((t // TILES) * PR, PR), PR)
 
     def multiply(logits, t):
-        logits[...] = dot_nt(wbuf[t % 4], mfull[1, chunk_rows(t)])
+        for part in range(2):
+            piece = slice(part * TILE // 2, (part + 1) * TILE // 2)
+            logits[piece, :] = dot_nt(wbuf[t % 4, piece], mfull[1, chunk_rows(t)])
 
     def absorb(logits, t):
         j = (t + TILES) % TILES
@@ -313,7 +349,7 @@
             x = logits[g * 8:(g + 1) * 8, :]
             blocks.append(jnp.where(last, -jnp.inf, x) if g * 8 < REPEAT else x)
         first = jnp.where(t < 0, 2 * VOCAB * 8, jnp.minimum(j * TILE, VOCAB - TILE))
-        offset = wanted[:, rows] - first - lax.broadcasted_iota(jnp.int32, (8, CR), 0)
+        offset = wanted[:, rows] - first - lax.broadcasted_iota(jnp.int32, (8, PR), 0)
         before = mrun[:, rows]
         tops = [before] + [None] * 3
         for g, x in enumerate(blocks):
@@ -338,7 +374,7 @@
         def step(i, carry):
             t = 2 * i
 
-            @pl.when(t + 2 < CHUNKS * TILES)
+            @pl.when(t + 2 < PASSES * TILES)
             def _():
                 tile_copy(t + 2).start()
                 tile_copy(t + 3).start()
@@ -353,31 +389,20 @@
             absorb(lg0, t)
             return carry
 
-        lax.fori_loop(0, CHUNKS * TILES // 2, step, 0)
-        absorb(lg1, CHUNKS * TILES - 1)
-
-    project(0)
-    project(1)
-    pair_sum(0, 0)
-    finish_sum(0, 0)
-    pair_sum(0, 1)
-    forward(0, 0)
-    complete(0, 0)
-    mlp(0)
-    pair_sum(1, 0)
-    finish_sum(0, 1)
-    finish_sum(1, 0)
-    forward(0, 1)
-    complete(0, 1)
-    mlp(1)
-    forward(1, 0)
-    complete(1, 0)
-    vocab((
-        (1, lambda: pair_sum(1, 1)),
-        (4, lambda: finish_sum(1, 1)),
-        (7, lambda: forward(1, 1)),
-        (8, lambda: complete(1, 1)),
-    ))
+        lax.fori_loop(0, PASSES * TILES // 2, step, 0)
+        absorb(lg1, PASSES * TILES - 1)
+
+    acts = {"O": project, "A": pair_sum, "R": relay, "B": finish_sum, "F": forward, "C": complete, "M": mlp}
+
+    def run(plan):
+        for name in plan.split():
+            if len(name) == 2:
+                acts[name[0]](int(name[1]))
+            else:
+                acts[name[0]](int(name[1]), int(name[2]))
+
+    run(BEFORE)
+    vocab([(at, functools.partial(run, plan)) for at, plan in enumerate(DURING)])
 
     tops = mrun[...]
     top = jnp.max(tops, axis=0, keepdims=True)
@@ -410,10 +435,13 @@
         for c in range(CHUNKS):
             first_copy(s, c).wait_send()
             mine = block_rows(c, core, chip)
-            for rel in range(4):
+            for rel in (0, 1, 3):
                 gather_copy(s, c, rel, mine).wait_send()
+            for i in range(6):
+                second_copy(s, c, i).wait_send()
+            for rel in range(2):
+                cross_copy(s, c, rel, far[rel]).wait_send()
             for rel in range(3):
-                second_copy(s, c, rel).wait_send()
                 forward_copy(s, c, rel, block_rows(c, core, far[rel])).wait_send()
     for off in range(1, 8):
         stat_copy(off).wait_send()
@@ -436,12 +464,12 @@
             pltpu.VMEM((2, ROWS // 2, DIM), BF16),
             pltpu.VMEM((2, ROWS // 2, DIM), BF16),
             pltpu.VMEM((2, ROWS // 2, DIM), BF16),
-            pltpu.VMEM((2, CHUNKS, 3, BR, DIM), BF16),
+            pltpu.VMEM((2, CHUNKS, 6, BR, HD_COLS), BF16),
             pltpu.VMEM((2, ROWS, DIM), BF16),
             pltpu.VMEM((ROWS // 8, DIM), BF16),
             pltpu.VMEM((CR, FFN), BF16),
-            pltpu.VMEM((TILE, CR), F32),
-            pltpu.VMEM((TILE, CR), F32),
+            pltpu.VMEM((TILE, PR), F32),
+            pltpu.VMEM((TILE, PR), F32),
             pltpu.VMEM((8, ROWS), F32),
             pltpu.VMEM((8, ROWS), F32),
             pltpu.VMEM((8, ROWS), F32),
@@ -451,12 +479,14 @@
             sem((4,)),
             sem((2, CHUNKS)),
             sem((2, CHUNKS)),
-            sem((2, CHUNKS, 3)),
-            sem((2, CHUNKS, 3)),
+            sem((2, CHUNKS, 6)),
+            sem((2, CHUNKS, 6)),
             sem((2, CHUNKS, 4)),
             sem((2, CHUNKS, 4)),
             sem((2, CHUNKS, 3)),
             sem((2, CHUNKS, 3)),
+            sem((2, CHUNKS, 2)),
+            sem((2, CHUNKS, 2)),
             sem((7,)),
             sem((7,)),
         ],

time: 212 us -> 205 us (0.967)
  Pallas kernels: 196 us -> 189 us
    pallas_call x1, Pallas kernels: 179 us -> 171 us  [layer(): pl.pallas_call(layer_kernel, in_specs=[vmem, vmem, hbm, vmem, hbm, hbm, h...]
where the time goes in v3:
time: 205 us
  Pallas kernels  189 us (92%)
  local copies, waits for them, and re-layouts  13.1 us (6%)
    pallas_call x1, Pallas kernels, layer(): pl.pallas_call(layer_kernel, in_specs=[vmem, vmem, hbm, vmem, hbm, hbm, h...  171 us
    pallas_call x1, Pallas kernels, attention(): pl.pallas_call(functools.partial(attention_kernel, group), grid_spec=spec...  17.6 us
    unnamed x36, local copies, waits for them, and re-layouts  11.5 us

profile of v3, /device:TPU:0, one launch (start us, length us, event | category | flops | bytes accessed | tf_op | source)
XLA Modules:
  0.0 204.5 jit_solution(3291350723570272866)
XLA Ops:
  0.6 0.0 copy-start.4
  0.6 0.0 copy-start.12
  0.7 0.0 copy-start.8
  0.7 0.0 copy-start.5
  0.7 0.0 copy-start.6
  0.7 0.0 copy-start.3
  0.7 0.0 copy-start.9
  0.7 0.0 copy-start.7
  0.7 0.0 copy-start.1
  0.7 1.8 copy.24
  2.6 2.5 %copy.25 = bf16[192,16,1,64]{3,1,0,2:T(8,128)(2,1)} copy(bf16[192,16,1,64]{0,3,2,1:T(8,128)(2,1)} %param.27) | data formatting | bytes 786432 | tf_op args[7]
  5.1 1.6 pad_maximum_fusion.kv_ref
  6.7 0.0 copy-done.12
  6.7 0.0 copy-start.13
  6.7 0.0 copy-start.14
  6.7 0.0 copy-done.4
  6.7 0.0 copy-done.8
  6.8 0.0 copy-done.5
  6.8 0.0 copy-done.6
  6.8 0.0 copy-done.3
  6.8 0.0 copy-done.9
  6.8 0.0 copy-done.7
  6.8 0.0 copy-done.1
  6.8 0.0 copy-start
  6.8 2.2 %copy-done = bf16[16,64,2048]{2,1,0:T(8,128)(2,1)S(1)} copy-done((bf16[16,64,2048]{2,1,0:T(8,128)(2,1)S(1)}, bf16[16,64,2048]{2,1,0:T(8,128)(2,1)}, u32[]{:S(2)}) %copy-start) | copy-done | bytes 4194328
  9.0 17.6 %attention.1 = (bf16[1024,256]{1,0:T(8,128)(2,1)S(1)}, bf16[192,16,128]{2,1,0:T(8,128)(2,1)S(1)}) custom-call(s32[16]{0:T(128)S(1)} %copy-done.9, s32[16,12]{1,0:T(8,128)S(1)} %copy-done.7, bf16[1024,2048]{1,0:T(8,128)(2,1)S(1)} %bitcast.12, s32[16,1,64]{2,1,0:T(1,128)S(1)} %bitcast.15, s32[16,64,64]{2,1,0:T(8,128)S(1)} %copy-done.3, ...), custom_call_target="tpu_custom_call" | custom-call | tf_op jit(solution)/shard_map/attention/pallas_call | solution.py:155
  26.6 0.0 copy-start.2
  26.7 0.8 copy-done.2
  27.4 0.0 copy-done.13
  27.4 0.6 broadcast_in_dim.20.mgain
  28.1 0.0 copy-done.14
  28.1 0.6 broadcast_in_dim.21.fgain
  28.7 171.4 %layer.1 = (f32[16,64]{1,0:T(8,128)}, f32[16,64]{1,0:T(8,128)}) custom-call(bf16[1024,256]{1,0:T(8,128)(2,1)} %copy-done.2, bf16[256,2048]{1,0:T(8,128)(2,1)} %wo.1, bf16[1024,2048]{1,0:T(8,128)(2,1)} %bitcast.11, bf16[1,2048]{1,0:T(2,128)(2,1)} %broadcast_in_dim.20.mgain, bf16[2048,1024]{1,0:T(8,128)(2,1)} %wg_hbm.1, bf16[2048,1024]{1,0:T(8,128)(2,1)} %wu_hbm.1, ...), custom_call_target="tpu_custom_call" | custom-call | tf_op jit(solution)/shard_map/layer/pallas_call | solution.py:454
  200.0 0.0 copy-start.11
  200.1 0.0 copy-start.10
  200.1 0.4 slice_bitcast_fusion
  200.4 1.5 copy.26
  201.9 1.5 copy.27
  203.3 0.0 copy-done.11
  203.3 0.6 copy.30
  203.9 0.0 copy-done.10
  203.9 0.6 copy.31
  (1 shorter events, 0.0 us)
Async XLA Ops:
  0.6 6.1 %copy-start.4 = (bf16[192,768]{1,0:T(8,128)(2,1)S(1)}, bf16[192,768]{1,0:T(8,128)(2,1)}, u32[]{:S(2)}) copy-start(bf16[192,768]{1,0:T(8,128)(2,1)} %constant.2.clone.table_ref) | copy-start | bytes 884740
  0.6 6.0 %copy-start.12 = (bf16[2048]{0:T(1024)(128)(2,1)S(1)}, bf16[2048]{0:T(1024)(128)(2,1)}, u32[]{:S(2)}) copy-start(bf16[2048]{0:T(1024)(128)(2,1)} %param.28) | copy-start | bytes 12292
  0.7 6.1 %copy-start.8 = (s32[16,64]{1,0:T(8,128)S(1)}, s32[16,64]{1,0:T(8,128)}, u32[]{:S(2)}) copy-start(s32[16,64]{1,0:T(8,128)} %param.22) | copy-start | bytes 12292
  0.7 6.1 %copy-start.5 = (bf16[2048,64]{0,1:T(8,128)(2,1)S(1)}, bf16[2048,64]{0,1:T(8,128)(2,1)}, u32[]{:S(2)}) copy-start(bf16[2048,64]{0,1:T(8,128)(2,1)} %param.30) | copy-start | bytes 786436
  0.7 6.1 %copy-start.6 = (bf16[2048,64]{0,1:T(8,128)(2,1)S(1)}, bf16[2048,64]{0,1:T(8,128)(2,1)}, u32[]{:S(2)}) copy-start(bf16[2048,64]{0,1:T(8,128)(2,1)} %param.31) | copy-start | bytes 786436
  0.7 6.1 %copy-start.3 = (s32[16,64,64]{2,1,0:T(8,128)S(1)}, s32[16,64,64]{2,1,0:T(8,128)}, u32[]{:S(2)}) copy-start(s32[16,64,64]{2,1,0:T(8,128)} %mask_ref.1) | copy-start | bytes 786436
  0.7 6.1 %copy-start.9 = (s32[16]{0:T(128)S(1)}, s32[16]{0:T(128)}, u32[]{:S(2)}) copy-start(s32[16]{0:T(128)} %ctx_ref.1) | copy-start | bytes 196
  0.7 6.1 %copy-start.7 = (s32[16,12]{1,0:T(8,128)S(1)}, s32[16,12]{1,0:T(8,128)}, u32[]{:S(2)}) copy-start(s32[16,12]{1,0:T(8,128)} %bt_ref.1) | copy-start | bytes 2308
  0.7 6.1 %copy-start.1 = (bf16[2048,256]{1,0:T(8,128)(2,1)S(1)}, bf16[2048,256]{1,0:T(8,128)(2,1)}, u32[]{:S(2)}) copy-start(bf16[2048,256]{1,0:T(8,128)(2,1)} %wq_ref.1) | copy-start | bytes 3145732
  6.7 20.8 %copy-start.13 = (bf16[2048]{0:T(1024)(128)(2,1)S(1)}, bf16[2048]{0:T(1024)(128)(2,1)}, u32[]{:S(2)}) copy-start(bf16[2048]{0:T(1024)(128)(2,1)} %param.33) | copy-start | bytes 12292
  6.7 21.3 %copy-start.14 = (bf16[2048]{0:T(1024)(128)(2,1)S(1)}, bf16[2048]{0:T(1024)(128)(2,1)}, u32[]{:S(2)}) copy-start(bf16[2048]{0:T(1024)(128)(2,1)} %param.37) | copy-start | bytes 12292
  6.8 2.2 %copy-start = (bf16[16,64,2048]{2,1,0:T(8,128)(2,1)S(1)}, bf16[16,64,2048]{2,1,0:T(8,128)(2,1)}, u32[]{:S(2)}) copy-start(bf16[16,64,2048]{2,1,0:T(8,128)(2,1)} %param.20) | copy-start | bytes 12582916
  26.6 0.8 copy-start.2
  200.0 3.3 %copy-start.11 = (f32[16,64]{1,0:T(8,128)S(1)}, f32[16,64]{1,0:T(8,128)}, u32[]{:S(2)}) copy-start(f32[16,64]{1,0:T(8,128)} %get-tuple-element.22) | copy-start | bytes 12292
  200.1 3.9 %copy-start.10 = (f32[16,64]{1,0:T(8,128)S(1)}, f32[16,64]{1,0:T(8,128)}, u32[]{:S(2)}) copy-start(f32[16,64]{1,0:T(8,128)} %get-tuple-element.23) | copy-start | bytes 12292

commit v4 on v3

--- a/solution.py
+++ b/solution.py
@@ -35,7 +35,7 @@
 BF16 = jnp.bfloat16
 
 
-BEFORE = "O0 O1 A00 A01 R00 R01 B00 B01 O2 O3 F00 A02 F01 C00 M0 C01 A10 M1 A11 R02 R10 B10 R11 B11 F10 F11 C10 C11"
+BEFORE = "G T0 T1 O0 T2 A00 T3 O1 T4 A01 R00 T5 B00 R01 T6 B01 T7 O2 O3 F00 A02 F01 S C00 M0 C01 A10 M1 A11 R02 R10 B10 R11 B11 F10 F11 C10 C11"
 DURING = ("B02 A03", "R03 F02", "B03 C02 M2", "F03 A12 C03 M3", "R12 A13", "B12 R13", "B13 F12", "C12 F13", "C13")
 
 
@@ -71,98 +71,9 @@
     return lax.dot_general(a, b, (((0,), (0,)), ((), ())), preferred_element_type=F32)
 
 
-def attention_kernel(group, ctx_ref, bt_ref, hid_ref, depth_ref, mask_ref, gain_ref, wq_ref, wk_ref, wv_ref, table_ref, kv_ref, att_ref, kvout_ref, old_ref):
-    step = pl.program_id(0)
-    normed = normalize(hid_ref[...].astype(F32), gain_ref[...].astype(F32))
-    q_all = dot(normed, wq_ref[...])
-    kv_all = dot_nt(normed, jnp.concatenate([wk_ref[...], wv_ref[...]], axis=0))
-    lane = lax.broadcasted_iota(jnp.int32, (1, 128), 1)
-    low = lane < 64
-    first = (lane % 64) < 32
-
-    def rope(values, cosine, sine):
-        swapped = jnp.where(first, pltpu.roll(values, 96, 1), pltpu.roll(values, 32, 1))
-        return values * cosine + swapped * sine
-
-    for i in range(group):
-        b = step * group + i
-        ctx = ctx_ref[b]
-        rows = slice(i * NODES, (i + 1) * NODES)
-        position = depth_ref[i] + ctx
-        hot = (lax.broadcasted_iota(jnp.int32, (SPAN, NODES), 0) == position).astype(F32).astype(BF16)
-        looked = dot_tn(hot, table_ref[...])
-        both = looked[:, :256] + looked[:, 256:512] + looked[:, 512:]
-        cosine, sine = both[:, :128], both[:, 128:]
-        q01 = (rope(q_all[rows, :128], cosine, sine) * 0.125).astype(BF16)
-        q23 = (rope(q_all[rows, 128:], cosine, sine) * 0.125).astype(BF16)
-        kv_new = rope(kv_all[rows], jnp.where(low, cosine, 1.0), jnp.where(low, sine, 0.0)).astype(BF16)
-        for p in range(PAGES):
-            old_ref[i, p * PAGE:(p + 1) * PAGE, :] = kv_ref[bt_ref[b, p]].astype(F32)
-        slot = lax.broadcasted_iota(jnp.int32, (SPAN, NODES), 0)
-        node = lax.broadcasted_iota(jnp.int32, (SPAN, NODES), 1)
-        place = (slot - node == ctx).astype(F32).astype(BF16)
-        shifted = dot(place, kv_new)
-        slot_col = lax.broadcasted_iota(jnp.int32, (SPAN, 128), 0)
-        fresh = (slot_col >= ctx) & (slot_col < ctx + NODES)
-        merged = jnp.where(fresh, shifted, old_ref[i])
-        merged16 = merged.astype(BF16)
-        for p in range(PAGES):
-            kvout_ref[bt_ref[b, p]] = merged16[p * PAGE:(p + 1) * PAGE]
-        turned = pltpu.roll(merged, 64, 1)
-        k_even = jnp.where(low, merged, 0.0).astype(BF16)
-        v_odd = jnp.where(low, 0.0, merged).astype(BF16)
-        v_even = jnp.where(low, turned, 0.0).astype(BF16)
-        k_odd = jnp.where(low, 0.0, turned).astype(BF16)
-        tree = dot_nt(mask_ref[i].astype(F32).astype(BF16), place)
-        slot_row = lax.broadcasted_iota(jnp.int32, (NODES, SPAN), 1)
-        seen = (slot_row < ctx) | (tree > 0.5)
-
-        def head(query, keys):
-            score = jnp.where(seen, dot_nt(query, keys), -jnp.inf)
-            weight = jnp.exp(score - jnp.max(score, axis=-1, keepdims=True))
-            return weight.astype(BF16), jnp.sum(weight, axis=-1, keepdims=True)
-
-        for pair, query in enumerate((q01, q23)):
-            w_even, t_even = head(query, k_even)
-            w_odd, t_odd = head(query, k_odd)
-            mixed = dot(w_even, v_even) + dot(w_odd, v_odd)
-            att_ref[rows, pair * 128:(pair + 1) * 128] = (mixed / jnp.where(low, t_even, t_odd)).astype(BF16)
-
-
-def attention(hidden, tree_mask, depth, ctx_len, block_table, kv_cache, attn_norm, w_q, w_k, w_v, table):
-    group = 4
-    grid = (hidden.shape[0] // (group * NODES),)
-    spec = pltpu.PrefetchScalarGridSpec(
-        num_scalar_prefetch=2,
-        grid=grid,
-        in_specs=[
-            pl.BlockSpec((group * NODES, DIM), lambda i, *_: (i, 0)),
-            pl.BlockSpec((group, 1, NODES), lambda i, *_: (i, 0, 0)),
-            pl.BlockSpec((group, NODES, NODES), lambda i, *_: (i, 0, 0)),
-            pl.BlockSpec((1, DIM), lambda i, *_: (0, 0)),
-            pl.BlockSpec((DIM, 256), lambda i, *_: (0, 0)),
-            pl.BlockSpec((HD, DIM), lambda i, *_: (0, 0)),
-            pl.BlockSpec((HD, DIM), lambda i, *_: (0, 0)),
-            pl.BlockSpec(table.shape, lambda i, *_: (0, 0)),
-            pl.BlockSpec(kv_cache.shape, lambda i, *_: (0, 0, 0)),
-        ],
-        out_specs=[
-            pl.BlockSpec((group * NODES, 256), lambda i, *_: (i, 0)),
-            pl.BlockSpec(kv_cache.shape, lambda i, *_: (0, 0, 0)),
-        ],
-        scratch_shapes=[pltpu.VMEM((group, SPAN, 128), F32)],
-    )
-    return pl.pallas_call(
-        functools.partial(attention_kernel, group),
-        grid_spec=spec,
-        out_shape=[jax.ShapeDtypeStruct((hidden.shape[0], 256), BF16), jax.ShapeDtypeStruct(kv_cache.shape, BF16)],
-        compiler_params=pltpu.CompilerParams(vmem_limit_bytes=40 * 2**20),
-        name="attention",
-    )(ctx_len, block_table, hidden, depth, tree_mask, attn_norm, w_q, w_k, w_v, table, kv_cache)
-
-
-def layer_kernel(att, wo, hid, mgain, wg_hbm, wu_hbm, wd_hbm, fgain, wlm, sid, ln_ref, lp_ref,
-                 wg, wu, wd, wbuf, psib, pown, s1buf, s2buf, mfull, hown, pact, lg0, lg1, mrun, srun, prun, wanted, stat,
+def layer_kernel(ctx_ref, hid, depth, mask, table_bt, sid, kc, vc, again, wq, wk, wv, table, wo, mgain, wg_hbm, wu_hbm, wd_hbm, fgain, wlm,
+                 ln_ref, lp_ref, kc_out, vc_out,
+                 att, pages, gk, gv, wg, wu, wd, wbuf, psib, pown, s1buf, s2buf, mfull, hown, pact, lg0, lg1, mrun, srun, prun, wanted, stat,
                  load_sem, tile_sem, s1_send, s1_recv, s2_send, s2_recv, ag_send, ag_recv, fw_send, fw_recv, cr_send, cr_recv, fin_send, fin_recv):
     me = lax.axis_index("tp")
     core = me % 2
@@ -195,7 +106,11 @@
         pltpu.make_async_copy(hid.at[pl.ds(pl.multiple_of(own_rows(c), BR), BR)], hown.at[pl.ds(c * BR, BR)], load_sem.at[3 + c])
         for c in range(CHUNKS)
     ]
-    for copy in hid_loads + loads:
+    half_loads = [
+        pltpu.make_async_copy(hid.at[pl.ds(h * PR, PR)], wbuf.at[2 + h, pl.ds(0, PR)], load_sem.at[3 + CHUNKS + h])
+        for h in range(2)
+    ]
+    for copy in half_loads + hid_loads + loads:
         copy.start()
 
     def tile_copy(t):
@@ -211,6 +126,87 @@
     for i in range(16):
         wanted[:, pl.ds(i * NODES, NODES)] = sid[pl.ds(i, 1)] - me * VOCAB
 
+    lane = lax.broadcasted_iota(jnp.int32, (1, 128), 1)
+    low = lane < HD
+    first_half = (lane % HD) < HD // 2
+
+    def slot_of(row):
+        return (row % 16) * PAGE + 2 * ((row % 128) // 16) + row // 128
+
+    def read_pages():
+        pages[...] = jnp.full_like(pages, -1)
+        for b in range(16):
+            pages[:, pl.ds(b * 16, PAGES)] = table_bt[pl.ds(b, 1)]
+        hot = (lax.broadcasted_iota(jnp.int32, (192, 256), 0) == pages[...]).astype(F32)
+        hot = hot.T.astype(BF16)
+        gk[...] = dot_nt(hot, kc[...]).astype(BF16)
+        gv[...] = dot_nt(hot, vc[...]).astype(BF16)
+
+    def write_pages():
+        hot = (lax.broadcasted_iota(jnp.int32, (192, 256), 0) == pages[...]).astype(F32)
+        hot = hot.T.astype(BF16)
+        kc_out[...] = dot_tn(gk[...], hot).astype(BF16)
+        vc_out[...] = dot_tn(gv[...], hot).astype(BF16)
+
+    def rope(values, cosine, sine):
+        swapped = jnp.where(first_half, pltpu.roll(values, 96, 1), pltpu.roll(values, 32, 1))
+        return values * cosine + swapped * sine
+
+    def attend(unit):
+        if unit % 4 == 0:
+            half_loads[unit // 4].wait()
+        at = (unit % 4) * 128
+        values = wbuf[2 + unit // 4, at:at + 128].astype(F32)
+        normed = normalize(values, again[...].astype(F32))
+        q_all = dot(normed, wq[...])
+        kv_all = dot_nt(normed, jnp.concatenate([wk[...], wv[...]], axis=0))
+        for i in range(2):
+            b = unit * 2 + i
+            ctx = ctx_ref[b]
+            rows = slice(i * NODES, (i + 1) * NODES)
+            hot = (lax.broadcasted_iota(jnp.int32, (SPAN, NODES), 0) == depth[b:b + 1] + ctx).astype(F32).astype(BF16)
+            looked = dot_tn(hot, table[...])
+            both = looked[:, :256] + looked[:, 256:512] + looked[:, 512:]
+            cosine, sine = both[:, :128], both[:, 128:]
+            q01 = (rope(q_all[rows, :128], cosine, sine) * 0.125).astype(BF16)
+            q23 = (rope(q_all[rows, 128:], cosine, sine) * 0.125).astype(BF16)
+            kv_new = rope(kv_all[rows], jnp.where(low, cosine, 1.0), jnp.where(low, sine, 0.0)).astype(BF16)
+            group = slice(b * 16, (b + 1) * 16)
+            old_k = jnp.concatenate([gk[group, g * 128:(g + 1) * 128] for g in range(8)], axis=0).astype(F32)
+            old_v = jnp.concatenate([gv[group, g * 128:(g + 1) * 128] for g in range(8)], axis=0).astype(F32)
+            turned_k = pltpu.roll(old_k, HD, 1)
+            turned_v = pltpu.roll(old_v, HD, 1)
+            slot = slot_of(lax.broadcasted_iota(jnp.int32, (256, NODES), 0))
+            place = (slot - lax.broadcasted_iota(jnp.int32, (256, NODES), 1) == ctx).astype(F32).astype(BF16)
+            shifted = dot(place, kv_new)
+            wide = slot_of(lax.broadcasted_iota(jnp.int32, (256, 128), 0))
+            fresh = (wide >= ctx) & (wide < ctx + NODES)
+            k_even = jnp.where(low, jnp.where(fresh, shifted, jnp.concatenate([old_k, turned_k], axis=0)), 0.0)
+            v_odd = jnp.where(low, 0.0, jnp.where(fresh, shifted, jnp.concatenate([turned_v, old_v], axis=0)))
+            k_odd = pltpu.roll(k_even, HD, 1)
+            v_even = pltpu.roll(v_odd, HD, 1)
+            new_k = jnp.where(low, k_even[:128], k_odd[128:]).astype(BF16)
+            new_v = jnp.where(low, v_even[:128], v_odd[128:]).astype(BF16)
+            for g in range(8):
+                gk[group, g * 128:(g + 1) * 128] = new_k[g * 16:(g + 1) * 16]
+                gv[group, g * 128:(g + 1) * 128] = new_v[g * 16:(g + 1) * 16]
+            keys = (k_even.astype(BF16), k_odd.astype(BF16))
+            v_even, v_odd = v_even.astype(BF16), v_odd.astype(BF16)
+            tree = dot_nt(mask[b].astype(F32).astype(BF16), place)
+            seen = (slot_of(lax.broadcasted_iota(jnp.int32, (NODES, 256), 1)) < ctx) | (tree > 0.5)
+
+            def head(query, key):
+                score = jnp.where(seen, dot_nt(query, key), -jnp.inf)
+                weight = jnp.exp(score - jnp.max(score, axis=-1, keepdims=True))
+                return weight.astype(BF16), jnp.sum(weight, axis=-1, keepdims=True)
+
+            for pair, query in enumerate((q01, q23)):
+                w_even, t_even = head(query, keys[0])
+                w_odd, t_odd = head(query, keys[1])
+                mixed = dot(w_even, v_even) + dot(w_odd, v_odd)
+                out = (mixed / jnp.where(low, t_even, t_odd)).astype(BF16)
+                att[b * NODES:(b + 1) * NODES, pair * 128:(pair + 1) * 128] = out
+
     def half_rows(c, which):
         return pl.ds(pl.multiple_of(c * CR + which * HALF, HALF), HALF)
 
@@ -218,14 +214,14 @@
         return pl.ds(c * HALF, HALF)
 
     def first_copy(s, c):
-        return remote(psib.at[s, slab(c)], s1buf.at[s, slab(c)], s1_send.at[s, c], s1_recv.at[s, c], sib)
+        return remote(psib.at[slab(c)], s1buf.at[s, slab(c)], s1_send.at[s, c], s1_recv.at[s, c], sib)
 
     def project(c):
-        psib[0, slab(c)] = dot(att[half_rows(c, 1 - core)], wo[...]).astype(BF16)
+        psib[slab(c)] = dot(att[half_rows(c, 1 - core)], wo[...]).astype(BF16)
         if c == 0:
             pl.semaphore_wait(barrier, 7)
         first_copy(0, c).start()
-        pown[0, slab(c)] = dot(att[half_rows(c, core)], wo[...]).astype(BF16)
+        pown[slab(c)] = dot(att[half_rows(c, core)], wo[...]).astype(BF16)
 
     first_cols = pl.ds(0, HD_COLS)
     last_cols = pl.ds(HD_COLS, HD_COLS)
@@ -237,11 +233,11 @@
         q = (far[0], far[2], far[1], far[2], far[1], far[0])[i]
         target = peer((0, 0, 1, 1, 1, 0)[i])
         cols = (first_cols, first_cols, last_cols, last_cols, first_cols, last_cols)[i]
-        return remote(pown.at[s, stored(c, q), cols], s2buf.at[s, c, i], s2_send.at[s, c, i], s2_recv.at[s, c, i], target)
+        return remote(pown.at[stored(c, q), cols], s2buf.at[s, c, i], s2_send.at[s, c, i], s2_recv.at[s, c, i], target)
 
     def pair_sum(s, c):
         first_copy(s, c).wait_recv()
-        pown[s, slab(c)] = (pown[s, slab(c)].astype(F32) + s1buf[s, slab(c)].astype(F32)).astype(BF16)
+        pown[slab(c)] = (pown[slab(c)].astype(F32) + s1buf[s, slab(c)].astype(F32)).astype(BF16)
         for i in (1, 3, 0, 2):
             second_copy(s, c, i).start()
 
@@ -249,7 +245,7 @@
         for i, q, cols in ((1, far[1], first_cols), (3, far[0], last_cols)):
             second_copy(s, c, i).wait_recv()
             rows = stored(c, q)
-            pown[s, rows, cols] = (pown[s, rows, cols].astype(F32) + s2buf[s, c, i].astype(F32)).astype(BF16)
+            pown[rows, cols] = (pown[rows, cols].astype(F32) + s2buf[s, c, i].astype(F32)).astype(BF16)
         for i in (4, 5):
             second_copy(s, c, i).start()
 
@@ -267,8 +263,8 @@
         for i in (0, 2, 4, 5):
             second_copy(s, c, i).wait_recv()
         rows = stored(c, chip)
-        left = pown[s, rows, first_cols].astype(F32) + s2buf[s, c, 0].astype(F32) + s2buf[s, c, 4].astype(F32)
-        right = pown[s, rows, last_cols].astype(F32) + s2buf[s, c, 2].astype(F32) + s2buf[s, c, 5].astype(F32)
+        left = pown[rows, first_cols].astype(F32) + s2buf[s, c, 0].astype(F32) + s2buf[s, c, 4].astype(F32)
+        right = pown[rows, last_cols].astype(F32) + s2buf[s, c, 2].astype(F32) + s2buf[s, c, 5].astype(F32)
         total = jnp.concatenate([left, right], axis=1)
         if s == 0:
             hid_loads[c].wait()
@@ -323,11 +319,14 @@
 
             def one(j, carry):
                 cols = pl.ds(pl.multiple_of(j * 512, 512), 512)
-                out[1, slab(c), cols] = dot(pact[rows], wd[:, cols]).astype(BF16)
+                out[slab(c), cols] = dot(pact[rows], wd[:, cols]).astype(BF16)
                 return carry
 
             lax.fori_loop(0, DIM // 512, one, 0)
 
+        first_copy(0, c).wait_send()
+        for i in range(6):
+            second_copy(0, c, i).wait_send()
         down(1 - core, psib)
         first_copy(1, c).start()
         down(core, pown)
@@ -392,14 +391,11 @@
         lax.fori_loop(0, PASSES * TILES // 2, step, 0)
         absorb(lg1, PASSES * TILES - 1)
 
-    acts = {"O": project, "A": pair_sum, "R": relay, "B": finish_sum, "F": forward, "C": complete, "M": mlp}
+    acts = {"G": read_pages, "S": write_pages, "T": attend, "O": project, "A": pair_sum, "R": relay, "B": finish_sum, "F": forward, "C": complete, "M": mlp}
 
     def run(plan):
         for name in plan.split():
-            if len(name) == 2:
-                acts[name[0]](int(name[1]))
-            else:
-                acts[name[0]](int(name[1]), int(name[2]))
+            acts[name[0]](*(int(digit) for digit in name[1:]))
 
     run(BEFORE)
     vocab([(at, functools.partial(run, plan)) for at, plan in enumerate(DURING)])
@@ -433,11 +429,12 @@
 
     for s in range(2):
         for c in range(CHUNKS):
-            first_copy(s, c).wait_send()
+            if s == 1:
+                first_copy(s, c).wait_send()
             mine = block_rows(c, core, chip)
             for rel in (0, 1, 3):
                 gather_copy(s, c, rel, mine).wait_send()
-            for i in range(6):
+            for i in range(6 if s == 1 else 0):
                 second_copy(s, c, i).wait_send()
             for rel in range(2):
                 cross_copy(s, c, rel, far[rel]).wait_send()
@@ -447,22 +444,27 @@
         stat_copy(off).wait_send()
 
 
-def layer(att, w_o, hidden, mlp_norm, w_gate, w_up, w_down, final_norm, w_lm, score_id):
+def layer(*operands):
     vmem = pl.BlockSpec(memory_space=pltpu.VMEM)
     hbm = pl.BlockSpec(memory_space=pl.ANY)
+    smem = pl.BlockSpec(memory_space=pltpu.SMEM)
     sem = pltpu.SemaphoreType.DMA
     return pl.pallas_call(
         layer_kernel,
-        in_specs=[vmem, vmem, hbm, vmem, hbm, hbm, hbm, vmem, hbm, vmem],
-        out_specs=[vmem, vmem],
-        out_shape=[jax.ShapeDtypeStruct((16, NODES), F32)] * 2,
+        in_specs=[smem, hbm] + [vmem] * 13 + [hbm] * 3 + [vmem, hbm],
+        out_specs=[vmem] * 4,
+        out_shape=[jax.ShapeDtypeStruct((16, NODES), F32)] * 2 + [jax.ShapeDtypeStruct((PAGE * HD, 192), BF16)] * 2,
         scratch_shapes=[
+            pltpu.VMEM((ROWS, 256), BF16),
+            pltpu.VMEM((1, 256), jnp.int32),
+            pltpu.VMEM((256, PAGE * HD), BF16),
+            pltpu.VMEM((256, PAGE * HD), BF16),
             pltpu.VMEM((DIM, FFN), BF16),
             pltpu.VMEM((DIM, FFN), BF16),
             pltpu.VMEM((FFN, DIM), BF16),
             pltpu.VMEM((4, TILE, DIM), BF16),
-            pltpu.VMEM((2, ROWS // 2, DIM), BF16),
-            pltpu.VMEM((2, ROWS // 2, DIM), BF16),
+            pltpu.VMEM((ROWS // 2, DIM), BF16),
+            pltpu.VMEM((ROWS // 2, DIM), BF16),
             pltpu.VMEM((2, ROWS // 2, DIM), BF16),
             pltpu.VMEM((2, CHUNKS, 6, BR, HD_COLS), BF16),
             pltpu.VMEM((2, ROWS, DIM), BF16),
@@ -475,7 +477,7 @@
             pltpu.VMEM((8, ROWS), F32),
             pltpu.VMEM((1, ROWS), jnp.int32),
             pltpu.VMEM((8, 8, ROWS), F32),
-            sem((3 + CHUNKS,)),
+            sem((5 + CHUNKS,)),
             sem((4,)),
             sem((2, CHUNKS)),
             sem((2, CHUNKS)),
@@ -492,17 +494,22 @@
         ],
         compiler_params=pltpu.CompilerParams(collective_id=0, has_side_effects=True, vmem_limit_bytes=63 * 2**20),
         name="layer",
-    )(att, w_o, hidden, mlp_norm, w_gate, w_up, w_down, final_norm, w_lm, score_id)
+    )(*operands)
 
 
 def solution(mesh):
     def group_step(hidden, tree_mask, depth, ctx_len, block_table, score_id, k_cache, v_cache, attn_norm, w_q, w_k, w_v, w_o, mlp_norm, w_gate, w_up, w_down, final_norm, w_lm):
-        flat = hidden.reshape(ROWS, DIM)
-        kv_cache = jnp.concatenate([k_cache[:, :, 0], v_cache[:, :, 0]], axis=-1)
-        table = jnp.asarray(rope_table())
-        att, kv_out = attention(flat, tree_mask, depth[:, None, :], ctx_len, block_table, kv_cache, attn_norm[None], w_q, w_k.T, w_v.T, table)
-        log_norm, log_prob = layer(att, w_o, flat, mlp_norm[None], w_gate, w_up, w_down, final_norm[None], w_lm.T, score_id)
-        return log_norm, log_prob, kv_out[:, :, None, :HD], kv_out[:, :, None, HD:]
+        def as_stored(cache):
+            return jnp.transpose(cache[:, :, 0, :], (1, 2, 0)).reshape(PAGE * HD, 192)
+
+        def as_given(cache):
+            return jnp.transpose(cache.reshape(PAGE, HD, 192), (2, 0, 1))[:, :, None, :]
+
+        log_norm, log_prob, k_out, v_out = layer(
+            ctx_len, hidden.reshape(ROWS, DIM), depth, tree_mask, block_table, score_id, as_stored(k_cache), as_stored(v_cache), attn_norm[None],
+            w_q, w_k.T, w_v.T, jnp.asarray(rope_table()), w_o, mlp_norm[None], w_gate, w_up, w_down, final_norm[None], w_lm.T,
+        )
+        return log_norm, log_prob, as_given(k_out), as_given(v_out)
 
     request_spec = P("dp", None, None)
     node_spec = P("dp", None)

time: 205 us -> 195 us (0.951)
  Pallas kernels: 189 us -> 183 us
  local copies, waits for them, and re-layouts: 13.1 us -> 10.2 us
    pallas_call x2 -> x1, Pallas kernels: 189 us -> 183 us  [layer(): pl.pallas_call(layer_kernel, in_specs=[smem, hbm] + [vmem] * 13 + [hbm] *...]
    unnamed x36 -> x4, local copies, waits for them, and re-layouts: 11.5 us -> 6.35 us
where the time goes in v4:
time: 195 us; the launch traced here: 194 us
  Pallas kernels  183 us (94%)
  local copies, waits for them, and re-layouts  10.2 us (5%)
    pallas_call x1, Pallas kernels, layer(): pl.pallas_call(layer_kernel, in_specs=[smem, hbm] + [vmem] * 13 + [hbm] *...  183 us
    unnamed x4, local copies, waits for them, and re-layouts  6.35 us

profile of v4, /device:TPU:0, one launch (start us, length us, event | category | flops | bytes accessed | tf_op | source)
XLA Modules:
  0.0 194.3 jit_solution(8968062382273970706)
XLA Ops:
  0.6 1.3 broadcast_in_dim.15.again
  1.9 1.3 broadcast_in_dim.16.mgain
  3.2 1.3 broadcast_in_dim.17.fgain
  4.5 183.5 %layer.1 = (f32[16,64]{1,0:T(8,128)}, f32[16,64]{1,0:T(8,128)}, bf16[1024,192]{1,0:T(8,128)(2,1)}, bf16[1024,192]{1,0:T(8,128)(2,1)}) custom-call(s32[16]{0:T(128)} %ctx_ref.1, bf16[1024,2048]{1,0:T(8,128)(2,1)} %bitcast.25, s32[16,64]{1,0:T(8,128)} %depth.1, s32[16,64,64]{2,1,0:T(8,128)} %mask.1, s32[16,12]{1,0:T(8,128)} %table_bt.1, s32[16,64]{1,0:T(8,128)} %sid.1, ...), custom_call_target="tpu_custom_call" | custom-call | tf_op jit(solution)/shard_map/layer/pallas_call | solution.py:452
  188.0 1.3 copy.28
  189.3 1.3 copy.29
  190.6 1.9 copy.30
  192.4 1.9 copy.31

commit v5 on v4

--- a/solution.py
+++ b/solution.py
@@ -23,6 +23,8 @@
 TILES = 16
 REPEAT = TILES * TILE - VOCAB
 LOWEST = -3e38
+UP = 512
+DOWN = 1024
 CHUNKS = 4
 PASSES = 2
 PR = ROWS // PASSES
@@ -35,8 +37,8 @@
 BF16 = jnp.bfloat16
 
 
-BEFORE = "G T0 T1 O0 T2 A00 T3 O1 T4 A01 R00 T5 B00 R01 T6 B01 T7 O2 O3 F00 A02 F01 S C00 M0 C01 A10 M1 A11 R02 R10 B10 R11 B11 F10 F11 C10 C11"
-DURING = ("B02 A03", "R03 F02", "B03 C02 M2", "F03 A12 C03 M3", "R12 A13", "B12 R13", "B13 F12", "C12 F13", "C13")
+BEFORE = "G T0 T1 O0 T2 A00 T3 O1 T4 R00 A01 T5 B00 T6 R01 T7 F00 B01 O2 O3 A02 C00 F01 R02 A03 M0 C01 A10 B02 R03 S M1 R10 A11 F02 B10 B03 R11 F10 B11 C02 F03 C10 F11 C11"
+DURING = ("M2", "A12 C03 M3", "R12 A13", "B12 R13", "F12 B13", "C12 F13", "", "C13")
 
 
 def rope_table():
@@ -73,7 +75,7 @@
 
 def layer_kernel(ctx_ref, hid, depth, mask, table_bt, sid, kc, vc, again, wq, wk, wv, table, wo, mgain, wg_hbm, wu_hbm, wd_hbm, fgain, wlm,
                  ln_ref, lp_ref, kc_out, vc_out,
-                 att, pages, gk, gv, wg, wu, wd, wbuf, psib, pown, s1buf, s2buf, mfull, hown, pact, lg0, lg1, mrun, srun, prun, wanted, stat,
+                 att, pages, gk, gv, kmid, vmid, wg, wu, wd, wbuf, part, s1buf, s2buf, mfull, hown, pact, lg0, lg1, mrun, srun, prun, wanted, stat,
                  load_sem, tile_sem, s1_send, s1_recv, s2_send, s2_recv, ag_send, ag_recv, fw_send, fw_recv, cr_send, cr_recv, fin_send, fin_recv):
     me = lax.axis_index("tp")
     core = me % 2
@@ -142,11 +144,18 @@
         gk[...] = dot_nt(hot, kc[...]).astype(BF16)
         gv[...] = dot_nt(hot, vc[...]).astype(BF16)
 
+    cache_copies = [
+        pltpu.make_async_copy(kmid, kc_out, load_sem.at[5 + CHUNKS]),
+        pltpu.make_async_copy(vmid, vc_out, load_sem.at[6 + CHUNKS]),
+    ]
+
     def write_pages():
         hot = (lax.broadcasted_iota(jnp.int32, (192, 256), 0) == pages[...]).astype(F32)
         hot = hot.T.astype(BF16)
-        kc_out[...] = dot_tn(gk[...], hot).astype(BF16)
-        vc_out[...] = dot_tn(gv[...], hot).astype(BF16)
+        kmid[...] = dot_tn(gk[...], hot).astype(BF16)
+        vmid[...] = dot_tn(gv[...], hot).astype(BF16)
+        for copy in cache_copies:
+            copy.start()
 
     def rope(values, cosine, sine):
         swapped = jnp.where(first_half, pltpu.roll(values, 96, 1), pltpu.roll(values, 32, 1))
@@ -214,30 +223,31 @@
         return pl.ds(c * HALF, HALF)
 
     def first_copy(s, c):
-        return remote(psib.at[slab(c)], s1buf.at[s, slab(c)], s1_send.at[s, c], s1_recv.at[s, c], sib)
+        return remote(part.at[half_rows(c, 1 - core)], s1buf.at[s, slab(c)], s1_send.at[s, c], s1_recv.at[s, c], sib)
 
     def project(c):
-        psib[slab(c)] = dot(att[half_rows(c, 1 - core)], wo[...]).astype(BF16)
+        rows = pl.ds(c * CR, CR)
+        part[rows] = dot(att[rows], wo[...]).astype(BF16)
         if c == 0:
             pl.semaphore_wait(barrier, 7)
         first_copy(0, c).start()
-        pown[slab(c)] = dot(att[half_rows(c, core)], wo[...]).astype(BF16)
 
     first_cols = pl.ds(0, HD_COLS)
     last_cols = pl.ds(HD_COLS, HD_COLS)
 
     def stored(c, q):
-        return pl.ds(pl.multiple_of(c * HALF + q * BR, BR), BR)
+        return pl.ds(pl.multiple_of(c * CR + core * HALF + q * BR, BR), BR)
 
     def second_copy(s, c, i):
         q = (far[0], far[2], far[1], far[2], far[1], far[0])[i]
         target = peer((0, 0, 1, 1, 1, 0)[i])
         cols = (first_cols, first_cols, last_cols, last_cols, first_cols, last_cols)[i]
-        return remote(pown.at[stored(c, q), cols], s2buf.at[s, c, i], s2_send.at[s, c, i], s2_recv.at[s, c, i], target)
+        return remote(part.at[stored(c, q), cols], s2buf.at[s, c, i], s2_send.at[s, c, i], s2_recv.at[s, c, i], target)
 
     def pair_sum(s, c):
         first_copy(s, c).wait_recv()
-        pown[slab(c)] = (pown[slab(c)].astype(F32) + s1buf[s, slab(c)].astype(F32)).astype(BF16)
+        rows = half_rows(c, core)
+        part[rows] = (part[rows].astype(F32) + s1buf[s, slab(c)].astype(F32)).astype(BF16)
         for i in (1, 3, 0, 2):
             second_copy(s, c, i).start()
 
@@ -245,7 +255,7 @@
         for i, q, cols in ((1, far[1], first_cols), (3, far[0], last_cols)):
             second_copy(s, c, i).wait_recv()
             rows = stored(c, q)
-            pown[rows, cols] = (pown[rows, cols].astype(F32) + s2buf[s, c, i].astype(F32)).astype(BF16)
+            part[rows, cols] = (part[rows, cols].astype(F32) + s2buf[s, c, i].astype(F32)).astype(BF16)
         for i in (4, 5):
             second_copy(s, c, i).start()
 
@@ -263,8 +273,8 @@
         for i in (0, 2, 4, 5):
             second_copy(s, c, i).wait_recv()
         rows = stored(c, chip)
-        left = pown[rows, first_cols].astype(F32) + s2buf[s, c, 0].astype(F32) + s2buf[s, c, 4].astype(F32)
-        right = pown[rows, last_cols].astype(F32) + s2buf[s, c, 2].astype(F32) + s2buf[s, c, 5].astype(F32)
+        left = part[rows, first_cols].astype(F32) + s2buf[s, c, 0].astype(F32) + s2buf[s, c, 4].astype(F32)
+        right = part[rows, last_cols].astype(F32) + s2buf[s, c, 2].astype(F32) + s2buf[s, c, 5].astype(F32)
         total = jnp.concatenate([left, right], axis=1)
         if s == 0:
             hid_loads[c].wait()
@@ -304,32 +314,28 @@
             for copy in loads:
                 copy.wait()
 
+        rows = pl.ds(c * CR, CR)
+
         def up(j, carry):
-            cols = pl.ds(pl.multiple_of(j * 256, 256), 256)
-            values = mfull[0, pl.ds(c * CR, CR)]
+            cols = pl.ds(pl.multiple_of(j * UP, UP), UP)
+            values = mfull[0, rows]
             gate = dot(values, wg[:, cols])
             upper = dot(values, wu[:, cols])
             pact[:, cols] = (gate * (1.0 / (1.0 + jnp.exp(-gate))) * upper).astype(BF16)
             return carry
 
-        lax.fori_loop(0, FFN // 256, up, 0)
-
-        def down(which, out):
-            rows = pl.ds(pl.multiple_of(which * HALF, HALF), HALF)
-
-            def one(j, carry):
-                cols = pl.ds(pl.multiple_of(j * 512, 512), 512)
-                out[slab(c), cols] = dot(pact[rows], wd[:, cols]).astype(BF16)
-                return carry
-
-            lax.fori_loop(0, DIM // 512, one, 0)
-
+        lax.fori_loop(0, FFN // UP, up, 0)
         first_copy(0, c).wait_send()
         for i in range(6):
             second_copy(0, c, i).wait_send()
-        down(1 - core, psib)
+
+        def down(j, carry):
+            cols = pl.ds(pl.multiple_of(j * DOWN, DOWN), DOWN)
+            part[rows, cols] = dot(pact[...], wd[:, cols]).astype(BF16)
+            return carry
+
+        lax.fori_loop(0, DIM // DOWN, down, 0)
         first_copy(1, c).start()
-        down(core, pown)
 
     def chunk_rows(t):
         return pl.ds(pl.multiple_of((t // TILES) * PR, PR), PR)
@@ -402,9 +408,11 @@
 
     tops = mrun[...]
     top = jnp.max(tops, axis=0, keepdims=True)
-    stat[0, 0:1] = top
-    stat[0, 1:2] = jnp.sum(srun[...] * jnp.exp(tops - top), axis=0, keepdims=True)
-    stat[0, 2:3] = jnp.sum(prun[...], axis=0, keepdims=True)
+    total = jnp.sum(srun[...] * jnp.exp(tops - top), axis=0, keepdims=True)
+    picked = jnp.sum(prun[...], axis=0, keepdims=True)
+    for k, values in enumerate((top, total, picked)):
+        for i in range(8):
+            stat[0, pl.ds(8 * k + i, 1)] = values[:, i * 128:(i + 1) * 128]
 
     def stat_copy(off):
         return remote(stat.at[0], stat.at[off], fin_send.at[off - 1], fin_recv.at[off - 1], (me + off) % 8)
@@ -413,19 +421,20 @@
         stat_copy(off).start()
     for off in range(1, 8):
         stat_copy(off).wait_recv()
-    top = stat[0, 0:1]
+    top = stat[0, 0:8]
     for off in range(1, 8):
-        top = jnp.maximum(top, stat[off, 0:1])
+        top = jnp.maximum(top, stat[off, 0:8])
     total = jnp.zeros_like(top)
     picked = jnp.zeros_like(top)
     for off in range(8):
-        total = total + stat[off, 1:2] * jnp.exp(stat[off, 0:1] - top)
-        picked = picked + stat[off, 2:3]
+        total = total + stat[off, 8:16] * jnp.exp(stat[off, 0:8] - top)
+        picked = picked + stat[off, 16:24]
     log_norm = top + jnp.log(total)
     log_prob = picked - log_norm
-    for i in range(16):
-        ln_ref[pl.ds(i, 1), :] = log_norm[:, i * NODES:(i + 1) * NODES]
-        lp_ref[pl.ds(i, 1), :] = log_prob[:, i * NODES:(i + 1) * NODES]
+    for ref, values in ((ln_ref, log_norm), (lp_ref, log_prob)):
+        for i in range(8):
+            ref[pl.ds(2 * i, 1), :] = values[i:i + 1, 0:NODES]
+            ref[pl.ds(2 * i + 1, 1), :] = values[i:i + 1, NODES:]
 
     for s in range(2):
         for c in range(CHUNKS):
@@ -442,6 +451,8 @@
                 forward_copy(s, c, rel, block_rows(c, core, far[rel])).wait_send()
     for off in range(1, 8):
         stat_copy(off).wait_send()
+    for copy in cache_copies:
+        copy.wait()
 
 
 def layer(*operands):
@@ -452,19 +463,20 @@
     return pl.pallas_call(
         layer_kernel,
         in_specs=[smem, hbm] + [vmem] * 13 + [hbm] * 3 + [vmem, hbm],
-        out_specs=[vmem] * 4,
+        out_specs=[vmem, vmem, hbm, hbm],
         out_shape=[jax.ShapeDtypeStruct((16, NODES), F32)] * 2 + [jax.ShapeDtypeStruct((PAGE * HD, 192), BF16)] * 2,
         scratch_shapes=[
             pltpu.VMEM((ROWS, 256), BF16),
             pltpu.VMEM((1, 256), jnp.int32),
             pltpu.VMEM((256, PAGE * HD), BF16),
             pltpu.VMEM((256, PAGE * HD), BF16),
+            pltpu.VMEM((PAGE * HD, 192), BF16),
+            pltpu.VMEM((PAGE * HD, 192), BF16),
             pltpu.VMEM((DIM, FFN), BF16),
             pltpu.VMEM((DIM, FFN), BF16),
             pltpu.VMEM((FFN, DIM), BF16),
             pltpu.VMEM((4, TILE, DIM), BF16),
-            pltpu.VMEM((ROWS // 2, DIM), BF16),
-            pltpu.VMEM((ROWS // 2, DIM), BF16),
+            pltpu.VMEM((ROWS, DIM), BF16),
             pltpu.VMEM((2, ROWS // 2, DIM), BF16),
             pltpu.VMEM((2, CHUNKS, 6, BR, HD_COLS), BF16),
             pltpu.VMEM((2, ROWS, DIM), BF16),
@@ -476,8 +488,8 @@
             pltpu.VMEM((8, ROWS), F32),
             pltpu.VMEM((8, ROWS), F32),
             pltpu.VMEM((1, ROWS), jnp.int32),
-            pltpu.VMEM((8, 8, ROWS), F32),
-            sem((5 + CHUNKS,)),
+            pltpu.VMEM((8, 24, 128), F32),
+            sem((7 + CHUNKS,)),
             sem((4,)),
             sem((2, CHUNKS)),
             sem((2, CHUNKS)),

time: 195 us -> 178 us (0.913)
  Pallas kernels: 183 us -> 167 us
    pallas_call x1, Pallas kernels: 183 us -> 167 us  [layer(): pl.pallas_call(layer_kernel, in_specs=[smem, hbm] + [vmem] * 13 + [hbm] *...]
where the time goes in v5:
time: 178 us
  Pallas kernels  167 us (94%)
  local copies, waits for them, and re-layouts  10.2 us (6%)
    pallas_call x1, Pallas kernels, layer(): pl.pallas_call(layer_kernel, in_specs=[smem, hbm] + [vmem] * 13 + [hbm] *...  167 us
    unnamed x4, local copies, waits for them, and re-layouts  6.35 us

profile of v5, /device:TPU:0, one launch (start us, length us, event | category | flops | bytes accessed | tf_op | source)
XLA Modules:
  0.0 177.8 jit_solution(12470321774554010726)
XLA Ops:
  0.6 1.3 broadcast_in_dim.15.again
  1.9 1.3 broadcast_in_dim.16.mgain
  3.2 1.3 broadcast_in_dim.17.fgain
  4.5 166.9 %layer.1 = (f32[16,64]{1,0:T(8,128)}, f32[16,64]{1,0:T(8,128)}, bf16[1024,192]{1,0:T(8,128)(2,1)}, bf16[1024,192]{1,0:T(8,128)(2,1)}) custom-call(s32[16]{0:T(128)} %ctx_ref.1, bf16[1024,2048]{1,0:T(8,128)(2,1)} %bitcast.25, s32[16,64]{1,0:T(8,128)} %depth.1, s32[16,64,64]{2,1,0:T(8,128)} %mask.1, s32[16,12]{1,0:T(8,128)} %table_bt.1, s32[16,64]{1,0:T(8,128)} %sid.1, ...), custom_call_target="tpu_custom_call" | custom-call | tf_op jit(solution)/shard_map/layer/pallas_call | solution.py:463
  171.4 1.3 copy.28
  172.7 1.3 copy.29
  174.0 1.9 %copy.30 = bf16[192,16,1,64]{0,3,2,1:T(8,128)(2,1)} copy(bf16[192,16,1,64]{0,3,2,1:T(8,128)(2,1)} %bitcast.29) | data formatting | bytes 786432
  175.9 1.9 %copy.31 = bf16[192,16,1,64]{0,3,2,1:T(8,128)(2,1)} copy(bf16[192,16,1,64]{0,3,2,1:T(8,128)(2,1)} %bitcast.28) | data formatting | bytes 786432

commit v6 on v5

--- a/solution.py
+++ b/solution.py
@@ -37,8 +37,8 @@
 BF16 = jnp.bfloat16
 
 
-BEFORE = "G T0 T1 O0 T2 A00 T3 O1 T4 R00 A01 T5 B00 T6 R01 T7 F00 B01 O2 O3 A02 C00 F01 R02 A03 M0 C01 A10 B02 R03 S M1 R10 A11 F02 B10 B03 R11 F10 B11 C02 F03 C10 F11 C11"
-DURING = ("M2", "A12 C03 M3", "R12 A13", "B12 R13", "F12 B13", "C12 F13", "", "C13")
+BEFORE = "G T0 T1 O0 T2 A00 T3 O1 T4 R00 A01 T5 B00 T6 R01 T7 F00 B01 O2 O3 A02 C00 F01 M0 R02 C01 A10 A03 M1 R10 A11 S B10 R11 F10 B11 R03 C10 F11 C11 B02 B03"
+DURING = ("", "F02", "F03 C02 M2", "A12 C03 M3", "R12 A13", "R13 B12", "B13", "F12 F13", "C12 C13")
 
 
 def rope_table():
@@ -108,11 +108,11 @@
         pltpu.make_async_copy(hid.at[pl.ds(pl.multiple_of(own_rows(c), BR), BR)], hown.at[pl.ds(c * BR, BR)], load_sem.at[3 + c])
         for c in range(CHUNKS)
     ]
-    half_loads = [
-        pltpu.make_async_copy(hid.at[pl.ds(h * PR, PR)], wbuf.at[2 + h, pl.ds(0, PR)], load_sem.at[3 + CHUNKS + h])
-        for h in range(2)
+    quarter_loads = [
+        pltpu.make_async_copy(hid.at[pl.ds(h * 256, 256)], wbuf.at[2 + h // 2, pl.ds(h % 2 * 256, 256)], load_sem.at[5 + CHUNKS + h])
+        for h in range(4)
     ]
-    for copy in half_loads + hid_loads + loads:
+    for copy in quarter_loads + hid_loads + loads:
         copy.start()
 
     def tile_copy(t):
@@ -145,8 +145,8 @@
         gv[...] = dot_nt(hot, vc[...]).astype(BF16)
 
     cache_copies = [
-        pltpu.make_async_copy(kmid, kc_out, load_sem.at[5 + CHUNKS]),
-        pltpu.make_async_copy(vmid, vc_out, load_sem.at[6 + CHUNKS]),
+        pltpu.make_async_copy(kmid, kc_out, load_sem.at[3 + CHUNKS]),
+        pltpu.make_async_copy(vmid, vc_out, load_sem.at[4 + CHUNKS]),
     ]
 
     def write_pages():
@@ -162,11 +162,11 @@
         return values * cosine + swapped * sine
 
     def attend(unit):
-        if unit % 4 == 0:
-            half_loads[unit // 4].wait()
+        if unit % 2 == 0:
+            quarter_loads[unit // 2].wait()
         at = (unit % 4) * 128
         values = wbuf[2 + unit // 4, at:at + 128].astype(F32)
-        normed = normalize(values, again[...].astype(F32))
+        normed = normalize(values, again[...].astype(F32)[None])
         q_all = dot(normed, wq[...])
         kv_all = dot_nt(normed, jnp.concatenate([wk[...], wv[...]], axis=0))
         for i in range(2):
@@ -282,7 +282,7 @@
         state = (hown[rows].astype(F32) + total.astype(BF16).astype(F32)).astype(BF16)
         if s == 0:
             hown[rows] = state
-        gain = (mgain if s == 0 else fgain)[...].astype(F32)
+        gain = (mgain if s == 0 else fgain)[...].astype(F32)[None]
         mine = block_rows(c, core, chip)
         mfull[s, mine] = normalize(state.astype(F32), gain)
         for rel in (0, 1, 3):
@@ -489,7 +489,7 @@
             pltpu.VMEM((8, ROWS), F32),
             pltpu.VMEM((1, ROWS), jnp.int32),
             pltpu.VMEM((8, 24, 128), F32),
-            sem((7 + CHUNKS,)),
+            sem((9 + CHUNKS,)),
             sem((4,)),
             sem((2, CHUNKS)),
             sem((2, CHUNKS)),
@@ -509,6 +509,21 @@
     )(*operands)
 
 
+def hand_over(results):
+    def kernel(*refs):
+        for source, target in zip(refs[:4], refs[4:]):
+            target[...] = source[...]
+
+    vmem = pl.BlockSpec(memory_space=pltpu.VMEM)
+    return pl.pallas_call(
+        kernel,
+        in_specs=[vmem] * 4,
+        out_specs=[vmem] * 4,
+        out_shape=[jax.ShapeDtypeStruct(x.shape, x.dtype) for x in results],
+        name="hand_over",
+    )(*results)
+
+
 def solution(mesh):
     def group_step(hidden, tree_mask, depth, ctx_len, block_table, score_id, k_cache, v_cache, attn_norm, w_q, w_k, w_v, w_o, mlp_norm, w_gate, w_up, w_down, final_norm, w_lm):
         def as_stored(cache):
@@ -517,10 +532,10 @@
         def as_given(cache):
             return jnp.transpose(cache.reshape(PAGE, HD, 192), (2, 0, 1))[:, :, None, :]
 
-        log_norm, log_prob, k_out, v_out = layer(
-            ctx_len, hidden.reshape(ROWS, DIM), depth, tree_mask, block_table, score_id, as_stored(k_cache), as_stored(v_cache), attn_norm[None],
-            w_q, w_k.T, w_v.T, jnp.asarray(rope_table()), w_o, mlp_norm[None], w_gate, w_up, w_down, final_norm[None], w_lm.T,
-        )
+        log_norm, log_prob, k_out, v_out = hand_over(layer(
+            ctx_len, hidden.reshape(ROWS, DIM), depth, tree_mask, block_table, score_id, as_stored(k_cache), as_stored(v_cache), attn_norm,
+            w_q, w_k.T, w_v.T, jnp.asarray(rope_table()), w_o, mlp_norm, w_gate, w_up, w_down, final_norm, w_lm.T,
+        ))
         return log_norm, log_prob, as_given(k_out), as_given(v_out)
 
     request_spec = P("dp", None, None)

time: 178 us -> 165 us (0.927)
  local copies, waits for them, and re-layouts: 10.2 us -> 0 us
  Pallas kernels: 167 us -> 164 us
    unnamed x4 -> x0, local copies, waits for them, and re-layouts: 6.35 us -> none
    pallas_call x1, Pallas kernels: 167 us -> 162 us  [layer(): pl.pallas_call(layer_kernel, in_specs=[smem, hbm] + [vmem] * 13 + [hbm] *...]
    broadcast_in_dim x3 -> x0, local copies, waits for them, and re-layouts: 3.87 us -> none  [the longest x1 1.29 us: group_step(): attn_norm[None]]
    pallas_call x0 -> x1, Pallas kernels: none -> 2.24 us  [hand_over(): pl.pallas_call(kernel, in_specs=[vmem] * 4, out_specs=[vmem] * 4, out_sha...]
where the time goes in v6:
time: 165 us
  Pallas kernels  164 us (99%)
    pallas_call x1, Pallas kernels, layer(): pl.pallas_call(layer_kernel, in_specs=[smem, hbm] + [vmem] * 13 + [hbm] *...  162 us

profile of v6, /device:TPU:0, one launch (start us, length us, event | category | flops | bytes accessed | tf_op | source)
XLA Modules:
  0.0 164.7 jit_solution(9504013793900326094)
XLA Ops:
  0.6 161.8 %layer.1 = (f32[16,64]{1,0:T(8,128)}, f32[16,64]{1,0:T(8,128)}, bf16[1024,192]{1,0:T(8,128)(2,1)}, bf16[1024,192]{1,0:T(8,128)(2,1)}) custom-call(s32[16]{0:T(128)} %ctx_ref.1, bf16[1024,2048]{1,0:T(8,128)(2,1)} %bitcast.25, s32[16,64]{1,0:T(8,128)} %depth.1, s32[16,64,64]{2,1,0:T(8,128)} %mask.1, s32[16,12]{1,0:T(8,128)} %table_bt.1, s32[16,64]{1,0:T(8,128)} %sid.1, ...), custom_call_target="tpu_custom_call" | custom-call | tf_op jit(solution)/shard_map/layer/pallas_call | solution.py:463
  162.5 2.2 %hand_over.1 = (f32[16,64]{1,0:T(8,128)}, f32[16,64]{1,0:T(8,128)}, bf16[1024,192]{1,0:T(8,128)(2,1)}, bf16[1024,192]{1,0:T(8,128)(2,1)}) custom-call(f32[16,64]{1,0:T(8,128)} %get-tuple-element.12.refs_0_, f32[16,64]{1,0:T(8,128)} %get-tuple-element.13.refs_1_, bf16[1024,192]{1,0:T(8,128)(2,1)} %get-tuple-element.14.refs_2_, ...), custom_call_target="tpu_custom_call" | custom-call | tf_op jit(solution)/shard_map/hand_over/pallas_call | solution.py:518

commit v7 on v6

--- a/solution.py
+++ b/solution.py
@@ -37,8 +37,9 @@
 BF16 = jnp.bfloat16
 
 
-BEFORE = "G T0 T1 O0 T2 A00 T3 O1 T4 R00 A01 T5 B00 T6 R01 T7 F00 B01 O2 O3 A02 C00 F01 M0 R02 C01 A10 A03 M1 R10 A11 S B10 R11 F10 B11 R03 C10 F11 C11 B02 B03"
-DURING = ("", "F02", "F03 C02 M2", "A12 C03 M3", "R12 A13", "R13 B12", "B13", "F12 F13", "C12 C13")
+BEFORE = "G T0 T1 O0 T2 A00 T3 O1 T4 A01 T5 B00 T6 R01 T7 F00 B01 O2 O3 D00 C00 F01 A02 M0 R02 D01 A10 A03 C01 M1 R10 A11 S B10 R11 F10 B11 R03 D10 F11 D11 B02 B03 C10 C11"
+DURING = ("", "F02 F03", "D02 D03 C02 M2", "A12 C03 M3", "R12 A13", "R13 B12", "B13", "F12 F13", "D12 D13 C12 C13")
+DIRECT = ((0, 0),)
 
 
 def rope_table():
@@ -75,7 +76,7 @@
 
 def layer_kernel(ctx_ref, hid, depth, mask, table_bt, sid, kc, vc, again, wq, wk, wv, table, wo, mgain, wg_hbm, wu_hbm, wd_hbm, fgain, wlm,
                  ln_ref, lp_ref, kc_out, vc_out,
-                 att, pages, gk, gv, kmid, vmid, wg, wu, wd, wbuf, part, s1buf, s2buf, mfull, hown, pact, lg0, lg1, mrun, srun, prun, wanted, stat,
+                 att, pages, ahead, wide, across, gk, gv, kmid, vmid, wg, wu, wd, wbuf, part, s1buf, s2buf, mfull, hown, pact, lg0, lg1, mrun, srun, prun, wanted, stat,
                  load_sem, tile_sem, s1_send, s1_recv, s2_send, s2_recv, ag_send, ag_recv, fw_send, fw_recv, cr_send, cr_recv, fin_send, fin_recv):
     me = lax.axis_index("tp")
     core = me % 2
@@ -133,10 +134,13 @@
     first_half = (lane % HD) < HD // 2
 
     def slot_of(row):
-        return (row % 16) * PAGE + 2 * ((row % 128) // 16) + row // 128
+        return (row & 15) * PAGE + ((row >> 3) & 14) + (row >> 7)
 
     def read_pages():
         pages[...] = jnp.full_like(pages, -1)
+        ahead[...] = slot_of(lax.broadcasted_iota(jnp.int32, (256, NODES), 0)) - lax.broadcasted_iota(jnp.int32, (256, NODES), 1)
+        wide[...] = slot_of(lax.broadcasted_iota(jnp.int32, (256, 128), 0))
+        across[...] = slot_of(lax.broadcasted_iota(jnp.int32, (NODES, 256), 1))
         for b in range(16):
             pages[:, pl.ds(b * 16, PAGES)] = table_bt[pl.ds(b, 1)]
         hot = (lax.broadcasted_iota(jnp.int32, (192, 256), 0) == pages[...]).astype(F32)
@@ -169,52 +173,62 @@
         normed = normalize(values, again[...].astype(F32)[None])
         q_all = dot(normed, wq[...])
         kv_all = dot_nt(normed, jnp.concatenate([wk[...], wv[...]], axis=0))
+        looks = []
+        for i in range(2):
+            hot = (lax.broadcasted_iota(jnp.int32, (SPAN, NODES), 0) == depth[unit * 2 + i:unit * 2 + i + 1] + ctx_ref[unit * 2 + i]).astype(F32).astype(BF16)
+            looks.append(dot_tn(hot, table[...]))
+        ready = []
         for i in range(2):
             b = unit * 2 + i
             ctx = ctx_ref[b]
             rows = slice(i * NODES, (i + 1) * NODES)
-            hot = (lax.broadcasted_iota(jnp.int32, (SPAN, NODES), 0) == depth[b:b + 1] + ctx).astype(F32).astype(BF16)
-            looked = dot_tn(hot, table[...])
+            looked = looks[i]
             both = looked[:, :256] + looked[:, 256:512] + looked[:, 512:]
             cosine, sine = both[:, :128], both[:, 128:]
             q01 = (rope(q_all[rows, :128], cosine, sine) * 0.125).astype(BF16)
             q23 = (rope(q_all[rows, 128:], cosine, sine) * 0.125).astype(BF16)
             kv_new = rope(kv_all[rows], jnp.where(low, cosine, 1.0), jnp.where(low, sine, 0.0)).astype(BF16)
+            place = (ahead[...] == ctx).astype(F32).astype(BF16)
+            shifted = dot(place, kv_new)
+            tree = dot_nt(mask[b].astype(F32).astype(BF16), place)
+            seen = (across[...] < ctx) | (tree > 0.5)
+            ready.append((b, ctx, q01, q23, shifted, seen))
+        scores, values = [], []
+        for b, ctx, q01, q23, shifted, seen in ready:
             group = slice(b * 16, (b + 1) * 16)
             old_k = jnp.concatenate([gk[group, g * 128:(g + 1) * 128] for g in range(8)], axis=0).astype(F32)
             old_v = jnp.concatenate([gv[group, g * 128:(g + 1) * 128] for g in range(8)], axis=0).astype(F32)
             turned_k = pltpu.roll(old_k, HD, 1)
             turned_v = pltpu.roll(old_v, HD, 1)
-            slot = slot_of(lax.broadcasted_iota(jnp.int32, (256, NODES), 0))
-            place = (slot - lax.broadcasted_iota(jnp.int32, (256, NODES), 1) == ctx).astype(F32).astype(BF16)
-            shifted = dot(place, kv_new)
-            wide = slot_of(lax.broadcasted_iota(jnp.int32, (256, 128), 0))
-            fresh = (wide >= ctx) & (wide < ctx + NODES)
+            fresh = (wide[...] >= ctx) & (wide[...] < ctx + NODES)
             k_even = jnp.where(low, jnp.where(fresh, shifted, jnp.concatenate([old_k, turned_k], axis=0)), 0.0)
             v_odd = jnp.where(low, 0.0, jnp.where(fresh, shifted, jnp.concatenate([turned_v, old_v], axis=0)))
             k_odd = pltpu.roll(k_even, HD, 1)
             v_even = pltpu.roll(v_odd, HD, 1)
+            keys = jnp.concatenate([k_even.astype(BF16), k_odd.astype(BF16)], axis=0)
+            values.append((k_even, k_odd, v_even, v_odd))
+            scores.append([dot_nt(q01, keys), dot_nt(q23, keys)])
+        weights = []
+        for (b, ctx, q01, q23, shifted, seen), pairs in zip(ready, scores):
+            masked = [jnp.where(seen, pair[:, h * 256:(h + 1) * 256], -jnp.inf) for pair in pairs for h in range(2)]
+            tops = [jnp.max(x, axis=-1, keepdims=True) for x in masked]
+            weights.append([jnp.exp(x - top) for x, top in zip(masked, tops)])
+        for item, parts, (k_even, k_odd, v_even, v_odd) in zip(ready, weights, values):
+            b = item[0]
+            both_v = jnp.concatenate([v_even.astype(BF16), v_odd.astype(BF16)], axis=0)
+            sums = [jnp.sum(x, axis=-1, keepdims=True) for x in parts]
+            for pair in range(2):
+                joined = jnp.concatenate([parts[2 * pair].astype(BF16), parts[2 * pair + 1].astype(BF16)], axis=1)
+                mixed = dot(joined, both_v)
+                out = (mixed / jnp.where(low, sums[2 * pair], sums[2 * pair + 1])).astype(BF16)
+                att[b * NODES:(b + 1) * NODES, pair * 128:(pair + 1) * 128] = out
+        for item, (k_even, k_odd, v_even, v_odd) in zip(ready, values):
+            group = slice(item[0] * 16, (item[0] + 1) * 16)
             new_k = jnp.where(low, k_even[:128], k_odd[128:]).astype(BF16)
             new_v = jnp.where(low, v_even[:128], v_odd[128:]).astype(BF16)
             for g in range(8):
                 gk[group, g * 128:(g + 1) * 128] = new_k[g * 16:(g + 1) * 16]
                 gv[group, g * 128:(g + 1) * 128] = new_v[g * 16:(g + 1) * 16]
-            keys = (k_even.astype(BF16), k_odd.astype(BF16))
-            v_even, v_odd = v_even.astype(BF16), v_odd.astype(BF16)
-            tree = dot_nt(mask[b].astype(F32).astype(BF16), place)
-            seen = (slot_of(lax.broadcasted_iota(jnp.int32, (NODES, 256), 1)) < ctx) | (tree > 0.5)
-
-            def head(query, key):
-                score = jnp.where(seen, dot_nt(query, key), -jnp.inf)
-                weight = jnp.exp(score - jnp.max(score, axis=-1, keepdims=True))
-                return weight.astype(BF16), jnp.sum(weight, axis=-1, keepdims=True)
-
-            for pair, query in enumerate((q01, q23)):
-                w_even, t_even = head(query, keys[0])
-                w_odd, t_odd = head(query, keys[1])
-                mixed = dot(w_even, v_even) + dot(w_odd, v_odd)
-                out = (mixed / jnp.where(low, t_even, t_odd)).astype(BF16)
-                att[b * NODES:(b + 1) * NODES, pair * 128:(pair + 1) * 128] = out
 
     def half_rows(c, which):
         return pl.ds(pl.multiple_of(c * CR + which * HALF, HALF), HALF)
@@ -239,16 +253,19 @@
         return pl.ds(pl.multiple_of(c * CR + core * HALF + q * BR, BR), BR)
 
     def second_copy(s, c, i):
-        q = (far[0], far[2], far[1], far[2], far[1], far[0])[i]
-        target = peer((0, 0, 1, 1, 1, 0)[i])
-        cols = (first_cols, first_cols, last_cols, last_cols, first_cols, last_cols)[i]
+        if (s, c) in DIRECT:
+            q, target, cols = far[i // 2], peer(i // 2), (first_cols, last_cols)[i % 2]
+        else:
+            q = (far[0], far[2], far[1], far[2], far[1], far[0])[i]
+            target = peer((0, 0, 1, 1, 1, 0)[i])
+            cols = (first_cols, first_cols, last_cols, last_cols, first_cols, last_cols)[i]
         return remote(part.at[stored(c, q), cols], s2buf.at[s, c, i], s2_send.at[s, c, i], s2_recv.at[s, c, i], target)
 
     def pair_sum(s, c):
         first_copy(s, c).wait_recv()
         rows = half_rows(c, core)
         part[rows] = (part[rows].astype(F32) + s1buf[s, slab(c)].astype(F32)).astype(BF16)
-        for i in (1, 3, 0, 2):
+        for i in (4, 5, 0, 1, 2, 3) if (s, c) in DIRECT else (1, 3, 0, 2):
             second_copy(s, c, i).start()
 
     def relay(s, c):
@@ -270,11 +287,16 @@
         return remote(mfull.at[s, rows], mfull.at[s, rows], fw_send.at[s, c, rel], fw_recv.at[s, c, rel], sib)
 
     def finish_sum(s, c):
-        for i in (0, 2, 4, 5):
+        direct = (s, c) in DIRECT
+        for i in range(6) if direct else (0, 2, 4, 5):
             second_copy(s, c, i).wait_recv()
         rows = stored(c, chip)
-        left = part[rows, first_cols].astype(F32) + s2buf[s, c, 0].astype(F32) + s2buf[s, c, 4].astype(F32)
-        right = part[rows, last_cols].astype(F32) + s2buf[s, c, 2].astype(F32) + s2buf[s, c, 5].astype(F32)
+        left = part[rows, first_cols].astype(F32)
+        for i in (0, 2, 4) if direct else (0, 4):
+            left = left + s2buf[s, c, i].astype(F32)
+        right = part[rows, last_cols].astype(F32)
+        for i in (1, 3, 5) if direct else (2, 5):
+            right = right + s2buf[s, c, i].astype(F32)
         total = jnp.concatenate([left, right], axis=1)
         if s == 0:
             hid_loads[c].wait()
@@ -301,10 +323,12 @@
             cross_copy(s, c, rel, far[rel]).start()
             forward_copy(s, c, rel, rows).start()
 
-    def complete(s, c):
+    def forward_far(s, c):
         for i in range(2):
             cross_copy(s, c, i, far[2]).wait_recv()
         forward_copy(s, c, 2, block_rows(c, core, far[2])).start()
+
+    def complete(s, c):
         gather_copy(s, c, 3, block_rows(c, 1 - core, chip)).wait_recv()
         for rel in range(3):
             forward_copy(s, c, rel, block_rows(c, 1 - core, far[rel])).wait_recv()
@@ -397,7 +421,7 @@
         lax.fori_loop(0, PASSES * TILES // 2, step, 0)
         absorb(lg1, PASSES * TILES - 1)
 
-    acts = {"G": read_pages, "S": write_pages, "T": attend, "O": project, "A": pair_sum, "R": relay, "B": finish_sum, "F": forward, "C": complete, "M": mlp}
+    acts = {"G": read_pages, "S": write_pages, "T": attend, "O": project, "A": pair_sum, "R": relay, "B": finish_sum, "F": forward, "D": forward_far, "C": complete, "M": mlp}
 
     def run(plan):
         for name in plan.split():
@@ -468,6 +492,9 @@
         scratch_shapes=[
             pltpu.VMEM((ROWS, 256), BF16),
             pltpu.VMEM((1, 256), jnp.int32),
+            pltpu.VMEM((256, NODES), jnp.int32),
+            pltpu.VMEM((256, 128), jnp.int32),
+            pltpu.VMEM((NODES, 256), jnp.int32),
             pltpu.VMEM((256, PAGE * HD), BF16),
             pltpu.VMEM((256, PAGE * HD), BF16),
             pltpu.VMEM((PAGE * HD, 192), BF16),

time: 165 us -> 160 us (0.970)
  Pallas kernels: 164 us -> 159 us
    pallas_call x1, Pallas kernels: 162 us -> 157 us  [layer(): pl.pallas_call(layer_kernel, in_specs=[smem, hbm] + [vmem] * 13 + [hbm] *...]
where the time goes in v7:
time: 160 us
  Pallas kernels  159 us (99%)
    pallas_call x1, Pallas kernels, layer(): pl.pallas_call(layer_kernel, in_specs=[smem, hbm] + [vmem] * 13 + [hbm] *...  157 us

profile of v7, /device:TPU:0, one launch (start us, length us, event | category | flops | bytes accessed | tf_op | source)
XLA Modules:
  0.0 159.7 jit_solution(8846752288183566876)
XLA Ops:
  0.6 156.8 %layer.1 = (f32[16,64]{1,0:T(8,128)}, f32[16,64]{1,0:T(8,128)}, bf16[1024,192]{1,0:T(8,128)(2,1)}, bf16[1024,192]{1,0:T(8,128)(2,1)}) custom-call(s32[16]{0:T(128)} %ctx_ref.1, bf16[1024,2048]{1,0:T(8,128)(2,1)} %bitcast.25, s32[16,64]{1,0:T(8,128)} %depth.1, s32[16,64,64]{2,1,0:T(8,128)} %mask.1, s32[16,12]{1,0:T(8,128)} %table_bt.1, s32[16,64]{1,0:T(8,128)} %sid.1, ...), custom_call_target="tpu_custom_call" | custom-call | tf_op jit(solution)/shard_map/layer/pallas_call | solution.py:487
  157.4 2.2 %hand_over.1 = (f32[16,64]{1,0:T(8,128)}, f32[16,64]{1,0:T(8,128)}, bf16[1024,192]{1,0:T(8,128)(2,1)}, bf16[1024,192]{1,0:T(8,128)(2,1)}) custom-call(f32[16,64]{1,0:T(8,128)} %get-tuple-element.12.refs_0_, f32[16,64]{1,0:T(8,128)} %get-tuple-element.13.refs_1_, bf16[1024,192]{1,0:T(8,128)(2,1)} %get-tuple-element.14.refs_2_, ...), custom_call_target="tpu_custom_call" | custom-call | tf_op jit(solution)/shard_map/hand_over/pallas_call | solution.py:545
